TPU v7x, 512 devices: a whole 4x4x16 slice. The times are simulated.
512 devices in a mesh: nodes: 128 (over z_hi, y, x, core), heads: 4 (over z_lo).
Axes of the slice: x: 4, y: 4, z: 16 (z_hi: 4, z_lo: 4; z = z_hi * 4 + z_lo), core: 2. Of those that a mesh axis runs over, the one named last changes fastest.
Arguments:
- grid_state: bfloat16 [131072, 1024], P('nodes', 'heads'), may hold values from -6 to 6
- mesh_state: bfloat16 [32768, 1024], P('nodes', 'heads'), may hold values from -6 to 6
- encoder_query: bfloat16 [1024, 512], P('nodes', 'heads'), may hold values from -0.1875 to 0.1875
- encoder_key: bfloat16 [1024, 512], P('nodes', 'heads'), may hold values from -0.1875 to 0.1875
- encoder_value: bfloat16 [1024, 512], P('nodes', 'heads'), may hold values from -0.1875 to 0.1875
- encoder_output: bfloat16 [512, 1024], P('heads', 'nodes'), may hold values from -0.25 to 0.25
- window_query: bfloat16 [1024, 512], P('nodes', 'heads'), may hold values from -0.1875 to 0.1875
- window_key: bfloat16 [1024, 512], P('nodes', 'heads'), may hold values from -0.1875 to 0.1875
- window_value: bfloat16 [1024, 512], P('nodes', 'heads'), may hold values from -0.1875 to 0.1875
- window_output: bfloat16 [512, 1024], P('heads', 'nodes'), may hold values from -0.25 to 0.25
- expand_weight: bfloat16 [1024, 2048], P('nodes', 'heads'), may hold values from -0.1875 to 0.1875
- shrink_weight: bfloat16 [2048, 1024], P('heads', 'nodes'), may hold values from -0.125 to 0.125
- decoder_query: bfloat16 [1024, 512], P('nodes', 'heads'), may hold values from -0.1875 to 0.1875
- decoder_key: bfloat16 [1024, 512], P('nodes', 'heads'), may hold values from -0.1875 to 0.1875
- decoder_value: bfloat16 [1024, 512], P('nodes', 'heads'), may hold values from -0.1875 to 0.1875
- decoder_output: bfloat16 [512, 1024], P('heads', 'nodes'), may hold values from -0.25 to 0.25
- encoder_blocks: int32 [256, 8], P('nodes'), may hold values from 0 to 1023, as said below
- encoder_count: int32 [256], P('nodes'), may hold values from 2 to 8, as said below
- window_offsets: int32 [256, 4], P('nodes'), may hold values from -2 to 2, as said below
- decoder_blocks: int32 [1024, 3], P('nodes'), may hold values from 0 to 255, as said below
- decoder_count: int32 [1024], P('nodes'), may hold values from 1 to 3, as said below
Outputs:
- grid_out: bfloat16 [131072, 1024], P('nodes', 'heads')
- mesh_out: bfloat16 [32768, 1024], P('nodes', 'heads')
Inputs may be any that keep to these rules, and one draw needn't show every extreme that they name: `encoder_blocks`: row m names 8 different grid blocks; each lies among the grid blocks of the index of nodes that holds mesh block m, or in the nearer half of the grid blocks of the index on either side. The first encoder_count[m] slots of row m are live; every mesh block held by the first or last eighth of the indices of nodes has all 8 slots live. `window_offsets`: each row holds 4 different offsets, the first of them 0. `decoder_blocks`: row g names 3 different mesh blocks; each lies among the mesh blocks of the index of nodes that holds grid block g, or is the one block next to them on either side. The first decoder_count[g] slots of row g are live; every grid block of the first index of nodes has all 3 slots live.
All inputs are finite; a program needn't handle non-finite values.
Results may differ from a plain program's by a relative error of at most 0.012.
Values may be sent and summed in bfloat16 or wider, within the bound.
No kernel may reach another device: no remote copies, remote signals or barrier semaphores. Data moves between devices by JAX's collectives and lax.ppermute only.
A program may use at most 64 MiB of HBM per device.

v0:
```python
import functools

import jax
import jax.numpy as jnp
from jax import lax
from jax.experimental import pallas as pl
from jax.experimental.pallas import tpu as pltpu
from jax.sharding import Mesh
from jax.sharding import PartitionSpec as P


HEAD_DIM = 64
TILE = 128
PAIR = 2 * HEAD_DIM
D = 1024
SCALE = HEAD_DIM ** (-0.5)
EPSILON = 1e-05
NODES = ("zh", "y", "x", "core")
F32 = jnp.float32
BF16 = jnp.bfloat16


def in_vmem():
    return pl.BlockSpec(memory_space=pltpu.VMEM)


def in_smem():
    return pl.BlockSpec(memory_space=pltpu.SMEM)


def in_any():
    return pl.BlockSpec(memory_space=pltpu.HBM)


def call(kernel, outs, specs, scratch=(), flops=1 << 28, room=12):
    return pl.pallas_call(
        kernel,
        out_shape=tuple(jax.ShapeDtypeStruct(shape, BF16) for shape in outs),
        in_specs=list(specs),
        out_specs=tuple(in_vmem() for _ in outs),
        scratch_shapes=list(scratch),
        compiler_params=pltpu.CompilerParams(vmem_limit_bytes=room << 20),
        cost_estimate=pl.CostEstimate(flops=flops, bytes_accessed=1 << 20, transcendentals=0),
    )


def mm(a, b):
    return jnp.dot(a, b, preferred_element_type=F32)


def mm_t(a, b):
    return lax.dot_general(a, b, (((1,), (1,)), ((), ())), preferred_element_type=F32)


def normalize(values):
    values = values.astype(F32)
    average = jnp.mean(values, axis=-1, keepdims=True)
    centred = values - average
    spread = jnp.mean(centred * centred, axis=-1, keepdims=True)
    return (centred * lax.rsqrt(spread + EPSILON)).astype(BF16)


def wide(ref):
    return jnp.concatenate([ref[k] for k in range(ref.shape[0])], axis=-1)


def pack_kernel(*refs):
    *sources, out = refs
    t = 0
    for source in sources:
        whole = source[...]
        for k in range(0, whole.shape[1], 128):
            for g in range(out.shape[0]):
                out[g, t] = whole[:, k : k + 128]
            t += 1


def regroup_kernel(counts, src, *outs):
    first = 0
    for out, members in zip(outs, counts):
        column = 0
        for count in members:
            for h in range(4):
                for k in range(count):
                    for z in range(4):
                        out[z, :, column : column + 128] = src[z * 4 + h, first + k]
                    column += 128
            first += count


class Chunk:
    def __init__(self, widths):
        self.starts, self.widths, at = [], widths, 0
        for width in widths:
            self.starts.append(at)
            at += width

    def copies(self, k, dst, mine, theirs, core, sems):
        start, width = self.starts[k], self.widths[k]
        made = []
        for z in range(4):
            for n, (src, half) in enumerate(((mine, core), (theirs, 1 - core))):
                made.append(
                    pltpu.make_async_copy(
                        src.at[:, z, :, pl.ds(start, width)],
                        dst.at[z, :, half],
                        sems.at[z * 2 + n],
                    )
                )
        return made


CHUNK_A = Chunk((512, 512, 512))
CHUNK_B = Chunk((512, 512, 512, 512, 512))
CHUNK_C = Chunk((2048, 2048, 512, 512, 512, 512))


def weight_scratch(chunk, members):
    return [pltpu.VMEM((4, 16, 2, 8, chunk.widths[m]), BF16) for m in members] + [
        pltpu.SemaphoreType.DMA((len(members), 8))
    ]


class Weights:
    def __init__(self, chunk, members, pos, mine, theirs, buffers, sems):
        core = pos[1]
        self.buffers = buffers
        self.made = [
            chunk.copies(m, buffers[n], mine, theirs, core, sems.at[n])
            for n, m in enumerate(members)
        ]
        for group in self.made:
            for copy in group:
                copy.start()

    def get(self, n):
        for copy in self.made[n]:
            copy.wait()
        buffer = self.buffers[n]
        return buffer.reshape(D, buffer.shape[-1])[...]


def softmax_mix(queries, keys, values, dead):
    scores = jnp.where(dead, -1e30, mm_t(queries, keys))
    weights = jnp.exp(scores - jnp.max(scores, axis=-1, keepdims=True))
    weights = weights * (1.0 / jnp.sum(weights, axis=-1, keepdims=True))
    return mm(weights.astype(BF16), values)


def two_heads(queries, keys, values, dead):
    first = lax.broadcasted_iota(jnp.int32, queries.shape, 1) < HEAD_DIM
    zero = jnp.zeros_like(queries)
    low = softmax_mix(jnp.where(first, queries, zero), keys, values, dead)
    high = softmax_mix(jnp.where(first, zero, queries), keys, values, dead)
    return jnp.where(first, low, high).astype(BF16)


def inputs_kernel(
    pos, x0, x1, x2, x3, mine, theirs, out0, out1, out2, out3, grid, mesh, staged, wk, wv, wq, sems
):
    weights = Weights(CHUNK_A, (0, 1, 2), pos, mine, theirs, (wk, wv, wq), sems)
    head = pos[2]
    rows, half = grid.shape[1], mesh.shape[1] // 2
    for k, part in enumerate((x0, x1, x2, x3)):
        grid[head ^ k] = part[:rows, :]
        mesh[head ^ k] = part[rows:, :]
    grid_norm = normalize(wide(grid))
    mesh_norm = normalize(wide(mesh))
    keys = mm(grid_norm, weights.get(0)).astype(BF16)
    for j in range(4):
        staged[j, :rows, :PAIR] = keys[:, j * PAIR : (j + 1) * PAIR]
    values = mm(grid_norm, weights.get(1)).astype(BF16)
    for j in range(4):
        staged[j, :rows, PAIR:] = values[:, j * PAIR : (j + 1) * PAIR]
    queries = (mm(mesh_norm, weights.get(2)) * SCALE).astype(BF16)
    for j in range(4):
        staged[j, rows:, :PAIR] = queries[:half, j * PAIR : (j + 1) * PAIR]
        staged[j, rows:, PAIR:] = queries[half:, j * PAIR : (j + 1) * PAIR]
    for k, out in enumerate((out0, out1, out2, out3)):
        out[...] = staged[head ^ k]


def arrange_kernel(pos, x0, x1, x2, x3, own, last, first):
    head = pos[2]
    for k, part in enumerate((x0, x1, x2, x3)):
        own[head ^ k] = part[...]
    last[...] = own[2:, :256, :]
    first[...] = own[:2, :256, :]


def encode_kernel(pos, blocks, count, own, before, after, out, tiles, picked):
    rows = own.shape[1] - 32
    for j in range(2):
        for k in range(2):
            part = slice(k * TILE, (k + 1) * TILE)
            tiles[j * 2 + k] = before[j, part]
            tiles[12 + j * 2 + k] = after[j, part]
    for j in range(4):
        for k in range(rows // TILE):
            tiles[4 + j * 2 + k] = own[j, k * TILE : (k + 1) * TILE]
    start = pos[0] * 8 - 4
    slots = blocks.shape[1]
    column = lax.broadcasted_iota(jnp.int32, (TILE, slots * TILE), 1)
    for m in range(2):
        for s in range(slots):
            index = jnp.clip(blocks[m, s] - start, 0, 15)
            picked[s * TILE : (s + 1) * TILE, :] = tiles[index]
        queries = jnp.concatenate(
            [
                own[2 * m + g, rows:, side * PAIR : (side + 1) * PAIR]
                for g in range(2)
                for side in range(2)
            ],
            axis=0,
        )
        mixed = two_heads(queries, picked[:, :PAIR], picked[:, PAIR:], column >= count[m] * TILE)
        out[2 * m] = mixed[:64]
        out[2 * m + 1] = mixed[64:]


def first_kernel(pos, encoded, mesh, mine, theirs, qkv, kept, wo, wq, wk, wv, sems):
    weights = Weights(CHUNK_B, (0, 1, 2, 3), pos, mine, theirs, (wo, wq, wk, wv), sems)
    update = mm_t(wide(encoded), weights.get(0))
    mesh_one = (wide(mesh).astype(F32) + update).astype(BF16)
    kept[...] = mesh_one
    norm_one = normalize(mesh_one)
    for n, scaling in enumerate((SCALE, 1.0, 1.0)):
        part = (mm(norm_one, weights.get(1 + n)) * scaling).astype(BF16)
        for j in range(4):
            qkv[j, :, n * PAIR : (n + 1) * PAIR] = part[:, j * PAIR : (j + 1) * PAIR]


def window_kernel(pos, offsets, own, before, after, out, tiles, picked):
    for j in range(4):
        half = slice((j % 2) * 64, (j % 2) * 64 + 64)
        tiles[j // 2, half] = before[j]
        tiles[2 + j // 2, half] = own[j, :, PAIR:]
        tiles[4 + j // 2, half] = after[j]
    slots = offsets.shape[1]
    slot = lax.broadcasted_iota(jnp.int32, (TILE, slots * TILE), 1) // TILE
    for m in range(2):
        alive = jnp.zeros((TILE, slots * TILE), jnp.int32)
        for s in range(slots):
            offset = offsets[m, s]
            picked[s * TILE : (s + 1) * TILE, :] = tiles[jnp.clip(m + 2 + offset, 0, 5)]
            reached = pos[0] * 2 + m + offset
            live = jnp.where((reached >= 0) & (reached < pos[3]), 1, 0)
            alive = jnp.where(slot == s, live, alive)
        queries = jnp.concatenate([own[2 * m, :, :PAIR], own[2 * m + 1, :, :PAIR]], axis=0)
        mixed = two_heads(queries, picked[:, :PAIR], picked[:, PAIR:], alive == 0)
        out[2 * m] = mixed[:64]
        out[2 * m + 1] = mixed[64:]


def second_kernel(
    pos, windowed, kept, mine_b, theirs_b, mine_c, theirs_c, mesh_out, kv, wo, up, down, wk, wv,
    sems_b, sems_c
):
    near = Weights(CHUNK_B, (4,), pos, mine_b, theirs_b, (wo,), sems_b)
    far = Weights(CHUNK_C, (0, 1, 2, 3), pos, mine_c, theirs_c, (up, down, wk, wv), sems_c)
    update = mm_t(wide(windowed), near.get(0))
    mesh_two = (kept[...].astype(F32) + update).astype(BF16)
    hidden = mm(normalize(mesh_two), far.get(0))
    hidden = (0.5 * hidden * (1.0 + lax.erf(hidden * (2.0**-0.5)))).astype(BF16)
    result = (mesh_two.astype(F32) + mm_t(hidden, far.get(1))).astype(BF16)
    for j in range(4):
        mesh_out[j] = result[:, j * 256 : (j + 1) * 256]
    norm_three = normalize(result)
    keys = mm(norm_three, far.get(2)).astype(BF16)
    values = mm(norm_three, far.get(3)).astype(BF16)
    for g in range(4):
        kv[g, :, :512] = keys
        kv[g, :, 512:] = values


def decode_kernel(pos, blocks, count, grid, own, before, after, mine, theirs, out, wq, wo, tiles,
                  picked, sems):
    weights = Weights(CHUNK_C, (4, 5), pos, mine, theirs, (wq, wo), sems)
    tiles[0] = before[...]
    for j in range(4):
        half = slice((j % 2) * 64, (j % 2) * 64 + 64)
        tiles[1 + j // 2, half] = own[j]
    tiles[3] = after[...]
    grid_rows = wide(grid)
    queries = (mm(normalize(grid_rows), weights.get(0)) * SCALE).astype(BF16)
    start = pos[0] * 2 - 1
    slots = blocks.shape[1]
    column = lax.broadcasted_iota(jnp.int32, (TILE, slots * TILE), 1)
    mixtures = []
    for t in range(2):
        row = pos[2] * 2 + t
        for s in range(slots):
            index = jnp.clip(blocks[row, s] - start, 0, 3)
            picked[s * TILE : (s + 1) * TILE, :] = tiles[index]
        dead = column >= count[row] * TILE
        mixtures.append(
            jnp.concatenate(
                [
                    two_heads(
                        queries[t * TILE : (t + 1) * TILE, j * PAIR : (j + 1) * PAIR],
                        picked[:, j * PAIR : (j + 1) * PAIR],
                        picked[:, 512 + j * PAIR : 512 + (j + 1) * PAIR],
                        dead,
                    )
                    for j in range(4)
                ],
                axis=1,
            )
        )
    decoded = jnp.concatenate(mixtures, axis=0)
    result = (grid_rows.astype(F32) + mm_t(decoded, weights.get(1))).astype(BF16)
    for j in range(4):
        out[j] = result[:, j * 256 : (j + 1) * 256]


def exchange(x):
    return lax.all_to_all(x, "heads", 0, 0, tiled=True)


def halo(last, first):
    size = lax.axis_size(NODES)
    up = [(i, i + 1) for i in range(size - 1)]
    down = [(j, i) for i, j in up]
    return lax.ppermute(last, NODES, up), lax.ppermute(first, NODES, down)


def after_it(x, other):
    return lax.optimization_barrier((x, other))[0]


def in_hbm(x):
    return pltpu.with_memory_space_constraint(x, pltpu.HBM)


def over_cores(x):
    return lax.ppermute(x, "core", [(0, 1), (1, 0)])


def trade(parts):
    out = [parts[0]]
    for k in range(1, 4):
        out.append(lax.ppermute(parts[k], "heads", [(i, i ^ k) for i in range(4)]))
    return out


def pack(sources):
    width = sum(w.shape[1] // 128 for w in sources)
    (tiles,) = call(
        pack_kernel, [(16, width, 8, 128)], [in_vmem()] * len(sources), room=56
    )(*sources)
    return tiles


def to_everyone(x):
    return jnp.broadcast_to(x[None], (16, *x.shape))


def over_plane(x):
    return lax.all_to_all(x, ("y", "x"), 0, 0, tiled=True)


def over_z(tiles, counts):
    arrived = lax.all_to_all(tiles, ("zh", "heads"), 0, 0, tiled=True)
    return call(
        functools.partial(regroup_kernel, counts),
        [(4, 8, 4 * sum(count) * 128) for count in counts],
        [in_vmem()],
    )(arrived)


def local(
    grid_state,
    mesh_state,
    encoder_query,
    encoder_key,
    encoder_value,
    encoder_output,
    window_query,
    window_key,
    window_value,
    window_output,
    expand_weight,
    shrink_weight,
    decoder_query,
    decoder_key,
    decoder_value,
    decoder_output,
    encoder_blocks,
    encoder_count,
    window_offsets,
    decoder_blocks,
    decoder_count,
):
    position = lax.axis_index(NODES)
    mesh_tiles = lax.axis_size(NODES) * 2
    pos = jnp.stack(
        [position, lax.axis_index("core"), lax.axis_index("heads"), jnp.int32(mesh_tiles)]
    ).astype(jnp.int32)

    counts = ((1, 1, 1), (1, 1, 1, 1, 1), (4, 4, 1, 1, 1, 1))
    tiles = pack(
        (
            encoder_key, encoder_value, encoder_query, encoder_output.T, window_query, window_key,
            window_value, window_output.T, expand_weight, shrink_weight.T, decoder_key,
            decoder_value, decoder_query, decoder_output.T,
        )
    )
    rows_a, rows_b, rows_c = over_z(tiles, counts)
    copies_a = to_everyone(rows_a)
    mine_a = over_plane(copies_a)
    theirs_a = over_cores(mine_a)
    mine_c = lax.all_gather(rows_c, ("y", "x"))

    head = lax.axis_index("heads")
    both = [
        jnp.concatenate(
            [
                lax.dynamic_index_in_dim(after_it(x, copies_a).reshape(4, -1, 256), head ^ k, 0, False)
                for x in (grid_state, mesh_state)
            ]
        )
        for k in range(4)
    ]
    *sent, grid, mesh = call(
        inputs_kernel,
        [(288, 256)] * 4 + [(4, 256, 256), (4, 64, 256)],
        [in_smem()] + [in_vmem()] * 4 + [in_any(), in_any()],
        [pltpu.VMEM((4, 288, 256), BF16)] + weight_scratch(CHUNK_A, (0, 1, 2)),
        room=16,
    )(pos, *trade(both), mine_a, theirs_a)
    copies_b = to_everyone(after_it(rows_b, mine_a))
    mine_b = over_plane(copies_b)
    own, last, first = call(
        arrange_kernel,
        [(4, 288, 256), (2, 256, 256), (2, 256, 256)],
        [in_smem()] + [in_vmem()] * 4,
        room=8,
    )(pos, *trade(sent))
    before, after = halo(last, first)
    theirs_b = over_cores(mine_b)
    mine_b, theirs_b = in_hbm(mine_b), in_hbm(theirs_b)
    (sent,) = call(
        encode_kernel,
        [(4, 64, 128)],
        [in_smem()] * 3 + [in_vmem()] * 3,
        [pltpu.VMEM((16, TILE, 256), BF16), pltpu.VMEM((8 * TILE, 256), BF16)],
    )(pos, encoder_blocks, encoder_count, own, before, after)
    encoded = exchange(sent)
    sent, kept = call(
        first_kernel,
        [(4, 64, 384), (64, D)],
        [in_smem(), in_vmem(), in_vmem(), in_any(), in_any()],
        weight_scratch(CHUNK_B, (0, 1, 2, 3)),
        room=16,
    )(pos, encoded, mesh, mine_b, theirs_b)
    own = exchange(sent)
    side = own[:, :, PAIR:]
    before, after = halo(side, side)
    mine_c = after_it(mine_c, (before, after))
    theirs_c = over_cores(mine_c)
    mine_c, theirs_c = in_hbm(mine_c), in_hbm(theirs_c)
    (sent,) = call(
        window_kernel,
        [(4, 64, 128)],
        [in_smem()] * 2 + [in_vmem()] * 3,
        [pltpu.VMEM((6, TILE, 256), BF16), pltpu.VMEM((4 * TILE, 256), BF16)],
    )(pos, window_offsets, own, before, after)
    windowed = exchange(sent)
    near, far = weight_scratch(CHUNK_B, (4,)), weight_scratch(CHUNK_C, (0, 1, 2, 3))
    sent, spread = call(
        second_kernel,
        [(4, 64, 256), (4, 64, D)],
        [in_smem(), in_vmem(), in_vmem()] + [in_any()] * 4,
        near[:-1] + far[:-1] + [near[-1], far[-1]],
        room=24,
    )(pos, windowed, kept, mine_b, theirs_b, mine_c, theirs_c)
    own = exchange(spread)
    mesh_out = exchange(sent).reshape(256, 256)
    before, after = halo(own[2:].reshape(TILE, D), own[:2].reshape(TILE, D))
    pair = weight_scratch(CHUNK_C, (4, 5))
    (sent,) = call(
        decode_kernel,
        [(4, 256, 256)],
        [in_smem()] * 3 + [in_vmem()] * 4 + [in_any()] * 2,
        pair[:-1]
        + [pltpu.VMEM((4, TILE, D), BF16), pltpu.VMEM((3 * TILE, D), BF16), pair[-1]],
        room=20,
    )(pos, decoder_blocks, decoder_count, grid, own, before, after, mine_c, theirs_c)
    grid_out = exchange(sent).reshape(1024, 256)
    return grid_out, mesh_out


def solution(mesh):
    sizes = (4, 4, 4, 2)
    fine = Mesh(mesh.devices.reshape(*sizes, mesh.devices.shape[1]), (*NODES, "heads"))
    both, flipped = P(NODES, "heads"), P("heads", NODES)
    in_specs = (
        both, both, both, both, both, flipped, both, both, both, flipped, both, flipped,
        both, both, both, flipped,
        P(NODES, None), P(NODES), P(NODES, None), P(NODES, None), P(NODES),
    )
    return jax.shard_map(
        local, mesh=fine, in_specs=in_specs, out_specs=(both, both), check_vma=False
    )
```

profile of v0, /device:TPU:31, one launch (start us, length us, event | category | flops | bytes accessed | tf_op | source)
XLA Modules:
  0.0 369.7 jit_solution(9159259729111314006)
XLA Ops:
  7.2 1.8 shard_map.212
  9.0 49.0 %all_to_all.45.src = bf16[16,20,8,128]{3,2,1,0:T(8,128)(2,1)S(1)} all-to-all(bf16[16,20,8,128]{3,2,1,0:T(8,128)(2,1)} %shard_map.212), channel_id=1, replica_groups=mesh['zh'=4,'y'=4,'x'=4,'core'=2,'heads'=4] {'zh','heads'}, dimensions={0} | all-to-all | bytes 1310720 | tf_op jit(solution)/shard_map/all_to_all | solution.py:363
  58.0 0.8 shard_map.213
  58.9 0.1 broadcast_in_dim.4
  59.0 25.5 %all_to_all.46.mine = bf16[16,4,8,1536]{3,2,1,0:T(8,128)(2,1)S(1)} all-to-all(bf16[16,4,8,1536]{3,2,1,0:T(8,128)(2,1)S(1)} %broadcast_in_dim.4), channel_id=1, replica_groups=mesh['zh'=4,'y'=4,'x'=4,'core'=2,'heads'=4] {'y','x'}, dimensions={0} | all-to-all | bytes 3145728 | tf_op jit(solution)/shard_map/all_to_all | solution.py:359
  84.6 0.2 broadcast_in_dim.5
  84.9 38.6 %all_to_all.47.mine.mine_b = bf16[16,4,8,2560]{3,2,1,0:T(8,128)(2,1)} all-to-all(bf16[16,4,8,2560]{3,2,1,0:T(8,128)(2,1)S(1)} %broadcast_in_dim.5), channel_id=1, replica_groups=mesh['zh'=4,'y'=4,'x'=4,'core'=2,'heads'=4] {'y','x'}, dimensions={0} | all-to-all | bytes 5242880 | tf_op jit(solution)/shard_map/all_to_all | solution.py:359
  123.5 23.8 %collective-permute-start.9 = (bf16[16,4,8,2560]{3,2,1,0:T(8,128)(2,1)}, bf16[16,4,8,2560]{3,2,1,0:T(8,128)(2,1)}, u32[]{:S(2)}, u32[]{:S(2)}) collective-permute-start(bf16[16,4,8,2560]{3,2,1,0:T(8,128)(2,1)} %all_to_all.47.mine.mine_b), channel_id=1, source_target_pairs={{0,4},{4,0},{1,5},{5,1},{2,6},{6,2},{3,7},{7,3},{8,12},{12,8},{9,1... | collective-permute-start | bytes 7864328 | tf_op jit(solution)/shard_map/ppermute | solution.py:336
  147.3 1.9 collective-permute-start.3
  149.3 1.1 dynamic-slice_bitcast_fusion
  150.4 9.8 %collective-permute-start.2 = (bf16[320,256]{1,0:T(8,128)(2,1)S(1)}, bf16[320,256]{1,0:T(8,128)(2,1)S(1)}, u32[]{:S(2)}, u32[]{:S(2)}) collective-permute-start(bf16[320,256]{1,0:T(8,128)(2,1)S(1)} %pad_maximum_fusion.3), channel_id=1, source_target_pairs={{0,3},{1,2},{2,1},{3,0},{4,7},{5,6},{6,5},{7,4},{8,11},{9,10},{10,... | collective-permute-start | bytes 491528 | tf_op jit(solution)/shard_map/ppermute | solution.py:342
  160.3 1.9 collective-permute-start.1
  162.3 2.2 collective-permute-start
  164.6 10.8 %collective-permute-done.1.x2 = bf16[320,256]{1,0:T(8,128)(2,1)S(1)} collective-permute-done((bf16[320,256]{1,0:T(8,128)(2,1)S(1)}, bf16[320,256]{1,0:T(8,128)(2,1)S(1)}, u32[]{:S(2)}, u32[]{:S(2)}) %collective-permute-start.1) | collective-permute-done | bytes 163872 | tf_op jit(solution)/shard_map/ppermute | solution.py:342
  175.4 2.9 shard_map.214
  178.4 1.9 collective-permute-start.4
  180.3 2.5 collective-permute-start.5
  182.8 4.8 %collective-permute-start.6 = (bf16[288,256]{1,0:T(8,128)(2,1)S(1)}, bf16[288,256]{1,0:T(8,128)(2,1)S(1)}, u32[]{:S(2)}, u32[]{:S(2)}) collective-permute-start(bf16[288,256]{1,0:T(8,128)(2,1)S(1)} %get-tuple-element.29), channel_id=1, source_target_pairs={{0,3},{1,2},{2,1},{3,0},{4,7},{5,6},{6,5},{7,4},{8,11},{9,10},{10,... | collective-permute-start | bytes 442376 | tf_op jit(solution)/shard_map/ppermute | solution.py:342
  187.7 6.7 %collective-permute-done.5.x2 = bf16[288,256]{1,0:T(8,128)(2,1)S(1)} collective-permute-done((bf16[288,256]{1,0:T(8,128)(2,1)S(1)}, bf16[288,256]{1,0:T(8,128)(2,1)S(1)}, u32[]{:S(2)}, u32[]{:S(2)}) %collective-permute-start.5) | collective-permute-done | bytes 147488 | tf_op jit(solution)/shard_map/ppermute | solution.py:342
  194.4 0.6 shard_map.215
  195.0 4.4 %collective-permute-start.7 = (bf16[2,256,256]{2,1,0:T(8,128)(2,1)S(1)}, bf16[2,256,256]{2,1,0:T(8,128)(2,1)S(1)}, u32[]{:S(2)}, u32[]{:S(2)}) collective-permute-start(bf16[2,256,256]{2,1,0:T(8,128)(2,1)S(1)} %get-tuple-element.31), channel_id=1, source_target_pairs={{0,4},{4,8},{8,12},{12,16},{16,20},{20,24},{24,28},{28,32},{32,36}... | collective-permute-start | bytes 786440 | tf_op jit(solution)/shard_map/ppermute | solution.py:324
  199.4 1.9 collective-permute-start.8
  201.3 1.4 collective-permute-done.7.before
  202.7 17.8 %collective-permute-done.8.after = bf16[2,256,256]{2,1,0:T(8,128)(2,1)S(1)} collective-permute-done((bf16[2,256,256]{2,1,0:T(8,128)(2,1)S(1)}, bf16[2,256,256]{2,1,0:T(8,128)(2,1)S(1)}, u32[]{:S(2)}, u32[]{:S(2)}) %collective-permute-start.8) | collective-permute-done | bytes 262176 | tf_op jit(solution)/shard_map/ppermute | solution.py:324
  220.4 2.6 shard_map.216
  223.1 9.4 %all_to_all.48.encoded = bf16[4,64,128]{2,1,0:T(8,128)(2,1)S(1)} all-to-all(bf16[4,64,128]{2,1,0:T(8,128)(2,1)S(1)} %shard_map.216), channel_id=1, replica_groups=mesh['zh'=4,'y'=4,'x'=4,'core'=2,'heads'=4] {'heads'}, dimensions={0} | all-to-all | bytes 131072 | tf_op jit(solution)/shard_map/all_to_all | solution.py:317
  232.5 3.7 shard_map.217
  236.2 8.0 %all_to_all.49.own = bf16[4,64,384]{2,1,0:T(8,128)(2,1)S(1)} all-to-all(bf16[4,64,384]{2,1,0:T(8,128)(2,1)S(1)} %get-tuple-element.36), channel_id=1, replica_groups=mesh['zh'=4,'y'=4,'x'=4,'core'=2,'heads'=4] {'heads'}, dimensions={0} | all-to-all | bytes 393216 | tf_op jit(solution)/shard_map/all_to_all | solution.py:317
  244.2 5.4 %collective-permute-start.10 = (bf16[4,64,256]{2,1,0:T(8,128)(2,1)S(1)}, bf16[4,64,256]{2,1,0:T(8,128)(2,1)S(1)}, u32[]{:S(2)}, u32[]{:S(2)}) collective-permute-start(bf16[4,64,256]{2,1,0:T(8,128)(2,1)S(1)} %slice.12), channel_id=1, source_target_pairs={{0,4},{4,8},{8,12},{12,16},{16,20},{20,24},{24,28},{28,32},{32,36}... | collective-permute-start | bytes 393224 | tf_op jit(solution)/shard_map/ppermute | solution.py:324
  249.7 1.9 collective-permute-start.11
  251.6 16.3 %collective-permute-done.11.after = bf16[4,64,256]{2,1,0:T(8,128)(2,1)S(1)} collective-permute-done((bf16[4,64,256]{2,1,0:T(8,128)(2,1)S(1)}, bf16[4,64,256]{2,1,0:T(8,128)(2,1)S(1)}, u32[]{:S(2)}, u32[]{:S(2)}) %collective-permute-start.11) | collective-permute-done | bytes 131104 | tf_op jit(solution)/shard_map/ppermute | solution.py:324
  267.9 1.9 collective-permute-start.12
  269.8 2.1 shard_map.218
  272.0 7.0 %all_to_all.50.windowed = bf16[4,64,128]{2,1,0:T(8,128)(2,1)S(1)} all-to-all(bf16[4,64,128]{2,1,0:T(8,128)(2,1)S(1)} %shard_map.218), channel_id=1, replica_groups=mesh['zh'=4,'y'=4,'x'=4,'core'=2,'heads'=4] {'heads'}, dimensions={0} | all-to-all | bytes 131072 | tf_op jit(solution)/shard_map/all_to_all | solution.py:317
  278.9 1.2 collective-permute-done.12.theirs_c.theirs
  280.2 2.6 copy-done.6
  282.8 9.2 %shard_map.219 = (bf16[4,64,256]{2,1,0:T(8,128)(2,1)}, bf16[4,64,1024]{2,1,0:T(8,128)(2,1)S(1)}) custom-call(s32[4]{0:T(128)S(1)} %pad_add_fusion.pos, bf16[4,64,128]{2,1,0:T(8,128)(2,1)S(1)} %all_to_all.50.windowed, bf16[64,1024]{1,0:T(8,128)(2,1)S(1)} %get-tuple-element.37.kept, bf16[16,4,8,2560]{3,2,1,0:T(8,128)(2,1)} %all_to_all.47.mine.mine_b, ...), custom_call_target="tpu_custom_call" | custom-call | flops 268435456 | bytes 1048576 | tf_op jit(solution)/shard_map/pallas_call | solution.py:470
  292.0 16.7 %all_to_all.51.own = bf16[4,64,1024]{2,1,0:T(8,128)(2,1)S(1)} all-to-all(bf16[4,64,1024]{2,1,0:T(8,128)(2,1)S(1)} %get-tuple-element.40), channel_id=1, replica_groups=mesh['zh'=4,'y'=4,'x'=4,'core'=2,'heads'=4] {'heads'}, dimensions={0} | all-to-all | bytes 1048576 | tf_op jit(solution)/shard_map/all_to_all | solution.py:317
  308.8 3.3 all-to-all-start.8
  312.1 2.6 collective-permute-start.13
  314.8 2.6 collective-permute-start.14
  317.5 0.6 collective-permute-done.13.before
  318.1 18.7 %collective-permute-done.14.after = bf16[128,1024]{1,0:T(8,128)(2,1)S(1)} collective-permute-done((bf16[128,1024]{1,0:T(8,128)(2,1)S(1)}, bf16[128,1024]{1,0:T(8,128)(2,1)S(1)}, u32[]{:S(2)}, u32[]{:S(2)}) %collective-permute-start.14) | collective-permute-done | bytes 262176 | tf_op jit(solution)/shard_map/ppermute | solution.py:324
  336.8 9.3 %shard_map.220 = bf16[4,256,256]{2,1,0:T(8,128)(2,1)} custom-call(s32[4]{0:T(128)S(1)} %pad_add_fusion.pos, s32[8,3]{1,0:T(8,128)S(1)} %copy.24.blocks, s32[8]{0:T(128)S(1)} %copy-done.4, bf16[4,256,256]{2,1,0:T(8,128)(2,1)S(1)} %copy-done.1, bf16[4,64,1024]{2,1,0:T(8,128)(2,1)S(1)} %all_to_all.51.own, bf16[128,1024]{1,0:T(8,128)(2,1)S(1)} %collective-permute-done.13.before, ...), custom_call_target="tpu_custom_call" | custom-call | flops 268435456 | bytes 1048576 | tf_op jit(solution)/shard_map/pallas_call | solution.py:481
  346.1 6.2 %all-to-all-start.7 = ((bf16[4,256,256]{2,1,0:T(8,128)(2,1)}), bf16[4,256,256]{2,1,0:T(8,128)(2,1)S(1)}, u32[]{:S(2)}, u32[]{:S(2)}) async-start(bf16[4,256,256]{2,1,0:T(8,128)(2,1)} %shard_map.220), calls=%async_computation.7 | async-start | bytes 1048576 | tf_op jit(solution)/shard_map/all_to_all | solution.py:317
  352.3 9.1 %all-to-all-done.7 = bf16[4,256,256]{2,1,0:T(8,128)(2,1)S(1)} async-done(((bf16[4,256,256]{2,1,0:T(8,128)(2,1)}), bf16[4,256,256]{2,1,0:T(8,128)(2,1)S(1)}, u32[]{:S(2)}, u32[]{:S(2)}) %all-to-all-start.7) | async-done | bytes 524320 | tf_op jit(solution)/shard_map/all_to_all | solution.py:317
  361.4 0.8 copy.27
  362.2 0.7 copy.28
  (37 shorter events, 0.4 us)
Async XLA Ops:
  7.2 260.7 %all-gather.3.cloned.1.call-start = ((), (), s32[]{:S(2)}) async-start(), calls=%async_computation.9 | async-start | bytes 6684672 | tf_op jit(solution)/shard_map/all_gather | solution.py:412
  84.8 64.4 %copy-start.7 = (bf16[256,256]{1,0:T(8,128)(2,1)S(1)}, bf16[256,256]{1,0:T(8,128)(2,1)}, u32[]{:S(2)}) copy-start(bf16[256,256]{1,0:T(8,128)(2,1)} %param.22) | copy-start | bytes 393220
  123.5 109.0 %collective-permute-start.9 = (bf16[16,4,8,2560]{3,2,1,0:T(8,128)(2,1)}, bf16[16,4,8,2560]{3,2,1,0:T(8,128)(2,1)}, u32[]{:S(2)}, u32[]{:S(2)}) collective-permute-start(bf16[16,4,8,2560]{3,2,1,0:T(8,128)(2,1)} %all_to_all.47.mine.mine_b), channel_id=1, source_target_pairs={{0,4},{4,0},{1,5},{5,1},{2,6},{6,2},{3,7},{7,3},{8,12},{12,8},{9,1... | collective-permute-start | bytes 7864328 | tf_op jit(solution)/shard_map/ppermute | solution.py:336
  147.3 28.1 %collective-permute-start.3 = (bf16[16,4,8,1536]{3,2,1,0:T(8,128)(2,1)S(1)}, bf16[16,4,8,1536]{3,2,1,0:T(8,128)(2,1)S(1)}, u32[]{:S(2)}, u32[]{:S(2)}) collective-permute-start(bf16[16,4,8,1536]{3,2,1,0:T(8,128)(2,1)S(1)} %all_to_all.46.mine), channel_id=1, source_target_pairs={{0,4},{4,0},{1,5},{5,1},{2,6},{6,2},{3,7},{7,3},{8,12},{12,8},{9,1... | collective-permute-start | bytes 4718600 | tf_op jit(solution)/shard_map/ppermute | solution.py:336
  150.4 14.1 %collective-permute-start.2 = (bf16[320,256]{1,0:T(8,128)(2,1)S(1)}, bf16[320,256]{1,0:T(8,128)(2,1)S(1)}, u32[]{:S(2)}, u32[]{:S(2)}) collective-permute-start(bf16[320,256]{1,0:T(8,128)(2,1)S(1)} %pad_maximum_fusion.3), channel_id=1, source_target_pairs={{0,3},{1,2},{2,1},{3,0},{4,7},{5,6},{6,5},{7,4},{8,11},{9,10},{10,... | collective-permute-start | bytes 491528 | tf_op jit(solution)/shard_map/ppermute | solution.py:342
  160.3 15.1 %collective-permute-start.1 = (bf16[320,256]{1,0:T(8,128)(2,1)S(1)}, bf16[320,256]{1,0:T(8,128)(2,1)S(1)}, u32[]{:S(2)}, u32[]{:S(2)}) collective-permute-start(bf16[320,256]{1,0:T(8,128)(2,1)S(1)} %pad_maximum_fusion.2), channel_id=1, source_target_pairs={{0,2},{1,3},{2,0},{3,1},{4,6},{5,7},{6,4},{7,5},{8,10},{9,11},{10,... | collective-permute-start | bytes 491528 | tf_op jit(solution)/shard_map/ppermute | solution.py:342
  162.3 58.2 %copy-start.2 = (s32[2,8]{1,0:T(2,128)S(1)}, s32[2,8]{1,0:T(2,128)}, u32[]{:S(2)}) copy-start(s32[2,8]{1,0:T(2,128)} %blocks.2) | copy-start | bytes 196
  162.3 58.2 %copy-start.3 = (s32[2]{0:T(128)S(1)}, s32[2]{0:T(128)}, u32[]{:S(2)}) copy-start(s32[2]{0:T(128)} %count.2) | copy-start | bytes 28
  162.3 13.1 %collective-permute-start = (bf16[320,256]{1,0:T(8,128)(2,1)S(1)}, bf16[320,256]{1,0:T(8,128)(2,1)S(1)}, u32[]{:S(2)}, u32[]{:S(2)}) collective-permute-start(bf16[320,256]{1,0:T(8,128)(2,1)S(1)} %pad_maximum_fusion.1), channel_id=1, source_target_pairs={{0,1},{1,0},{2,3},{3,2},{4,5},{5,4},{6,7},{7,6},{8,9},{9,8},{10,11... | collective-permute-start | bytes 491528 | tf_op jit(solution)/shard_map/ppermute | solution.py:342
  178.4 57.8 %copy-start = (bf16[4,256,256]{2,1,0:T(8,128)(2,1)}, bf16[4,256,256]{2,1,0:T(8,128)(2,1)S(1)}, u32[]{:S(2)}) copy-start(bf16[4,256,256]{2,1,0:T(8,128)(2,1)S(1)} %get-tuple-element.25.grid) | copy-start | bytes 1572868
  178.4 9.3 %collective-permute-start.4 = (bf16[288,256]{1,0:T(8,128)(2,1)S(1)}, bf16[288,256]{1,0:T(8,128)(2,1)S(1)}, u32[]{:S(2)}, u32[]{:S(2)}) collective-permute-start(bf16[288,256]{1,0:T(8,128)(2,1)S(1)} %get-tuple-element.27), channel_id=1, source_target_pairs={{0,1},{1,0},{2,3},{3,2},{4,5},{5,4},{6,7},{7,6},{8,9},{9,8},{10,11... | collective-permute-start | bytes 442376 | tf_op jit(solution)/shard_map/ppermute | solution.py:342
  180.3 14.1 %collective-permute-start.5 = (bf16[288,256]{1,0:T(8,128)(2,1)S(1)}, bf16[288,256]{1,0:T(8,128)(2,1)S(1)}, u32[]{:S(2)}, u32[]{:S(2)}) collective-permute-start(bf16[288,256]{1,0:T(8,128)(2,1)S(1)} %get-tuple-element.28), channel_id=1, source_target_pairs={{0,2},{1,3},{2,0},{3,1},{4,6},{5,7},{6,4},{7,5},{8,10},{9,11},{10,... | collective-permute-start | bytes 442376 | tf_op jit(solution)/shard_map/ppermute | solution.py:342
  182.8 11.5 %collective-permute-start.6 = (bf16[288,256]{1,0:T(8,128)(2,1)S(1)}, bf16[288,256]{1,0:T(8,128)(2,1)S(1)}, u32[]{:S(2)}, u32[]{:S(2)}) collective-permute-start(bf16[288,256]{1,0:T(8,128)(2,1)S(1)} %get-tuple-element.29), channel_id=1, source_target_pairs={{0,3},{1,2},{2,1},{3,0},{4,7},{5,6},{6,5},{7,4},{8,11},{9,10},{10,... | collective-permute-start | bytes 442376 | tf_op jit(solution)/shard_map/ppermute | solution.py:342
  195.0 7.7 %collective-permute-start.7 = (bf16[2,256,256]{2,1,0:T(8,128)(2,1)S(1)}, bf16[2,256,256]{2,1,0:T(8,128)(2,1)S(1)}, u32[]{:S(2)}, u32[]{:S(2)}) collective-permute-start(bf16[2,256,256]{2,1,0:T(8,128)(2,1)S(1)} %get-tuple-element.31), channel_id=1, source_target_pairs={{0,4},{4,8},{8,12},{12,16},{16,20},{20,24},{24,28},{28,32},{32,36}... | collective-permute-start | bytes 786440 | tf_op jit(solution)/shard_map/ppermute | solution.py:324
  199.4 21.1 %collective-permute-start.8 = (bf16[2,256,256]{2,1,0:T(8,128)(2,1)S(1)}, bf16[2,256,256]{2,1,0:T(8,128)(2,1)S(1)}, u32[]{:S(2)}, u32[]{:S(2)}) collective-permute-start(bf16[2,256,256]{2,1,0:T(8,128)(2,1)S(1)} %get-tuple-element.32), channel_id=1, source_target_pairs={{4,0},{8,4},{12,8},{16,12},{20,16},{24,20},{28,24},{32,28},{36,32}... | collective-permute-start | bytes 786440 | tf_op jit(solution)/shard_map/ppermute | solution.py:324
  232.5 37.3 %copy-start.5 = (s32[2,4]{1,0:T(2,128)S(1)}, s32[2,4]{1,0:T(2,128)}, u32[]{:S(2)}) copy-start(s32[2,4]{1,0:T(2,128)} %offsets.1) | copy-start | bytes 100
  244.2 7.4 %collective-permute-start.10 = (bf16[4,64,256]{2,1,0:T(8,128)(2,1)S(1)}, bf16[4,64,256]{2,1,0:T(8,128)(2,1)S(1)}, u32[]{:S(2)}, u32[]{:S(2)}) collective-permute-start(bf16[4,64,256]{2,1,0:T(8,128)(2,1)S(1)} %slice.12), channel_id=1, source_target_pairs={{0,4},{4,8},{8,12},{12,16},{16,20},{20,24},{24,28},{28,32},{32,36}... | collective-permute-start | bytes 393224 | tf_op jit(solution)/shard_map/ppermute | solution.py:324
  249.7 18.2 %collective-permute-start.11 = (bf16[4,64,256]{2,1,0:T(8,128)(2,1)S(1)}, bf16[4,64,256]{2,1,0:T(8,128)(2,1)S(1)}, u32[]{:S(2)}, u32[]{:S(2)}) collective-permute-start(bf16[4,64,256]{2,1,0:T(8,128)(2,1)S(1)} %slice.12), channel_id=1, source_target_pairs={{4,0},{8,4},{12,8},{16,12},{20,16},{24,20},{28,24},{32,28},{36,32}... | collective-permute-start | bytes 393224 | tf_op jit(solution)/shard_map/ppermute | solution.py:324
  267.9 12.3 %collective-permute-start.12 = (bf16[16,4,8,6144]{3,2,1,0:T(8,128)(2,1)}, bf16[16,4,8,6144]{3,2,1,0:T(8,128)(2,1)S(1)}, u32[]{:S(2)}, u32[]{:S(2)}) collective-permute-start(bf16[16,4,8,6144]{3,2,1,0:T(8,128)(2,1)} %bitcast.30), channel_id=1, source_target_pairs={{0,4},{4,0},{1,5},{5,1},{2,6},{6,2},{3,7},{7,3},{8,12},{12,8},{9,1... | collective-permute-start | bytes 18874376 | tf_op jit(solution)/shard_map/ppermute | solution.py:336
  280.2 2.6 copy-start.6
  282.8 34.6 %copy-start.8 = (s32[8,3]{0,1:T(4,128)S(1)}, s32[8,3]{0,1:T(4,128)}, u32[]{:S(2)}) copy-start(s32[8,3]{0,1:T(4,128)} %param.40) | copy-start | bytes 292
  282.8 54.0 %copy-start.4 = (s32[8]{0:T(128)S(1)}, s32[8]{0:T(128)}, u32[]{:S(2)}) copy-start(s32[8]{0:T(128)} %count.3) | copy-start | bytes 100
  292.0 44.8 %copy-start.1 = (bf16[4,256,256]{2,1,0:T(8,128)(2,1)S(1)}, bf16[4,256,256]{2,1,0:T(8,128)(2,1)}, u32[]{:S(2)}) copy-start(bf16[4,256,256]{2,1,0:T(8,128)(2,1)} %copy-done) | copy-start | bytes 1572868
  308.8 37.3 %all-to-all-start.8 = ((bf16[4,64,256]{2,1,0:T(8,128)(2,1)}), bf16[4,64,256]{2,1,0:T(8,128)(2,1)S(1)}, u32[]{:S(2)}, u32[]{:S(2)}) async-start(bf16[4,64,256]{2,1,0:T(8,128)(2,1)} %get-tuple-element.41), calls=%async_computation.8 | async-start | bytes 262144 | tf_op jit(solution)/shard_map/all_to_all | solution.py:317
  312.1 6.0 %collective-permute-start.13 = (bf16[128,1024]{1,0:T(8,128)(2,1)S(1)}, bf16[128,1024]{1,0:T(8,128)(2,1)S(1)}, u32[]{:S(2)}, u32[]{:S(2)}) collective-permute-start(bf16[128,1024]{1,0:T(8,128)(2,1)S(1)} %bitcast.37), channel_id=1, source_target_pairs={{0,4},{4,8},{8,12},{12,16},{16,20},{20,24},{24,28},{28,32},{32,36}... | collective-permute-start | bytes 786440 | tf_op jit(solution)/shard_map/ppermute | solution.py:324
  314.8 22.0 %collective-permute-start.14 = (bf16[128,1024]{1,0:T(8,128)(2,1)S(1)}, bf16[128,1024]{1,0:T(8,128)(2,1)S(1)}, u32[]{:S(2)}, u32[]{:S(2)}) collective-permute-start(bf16[128,1024]{1,0:T(8,128)(2,1)S(1)} %bitcast.36), channel_id=1, source_target_pairs={{4,0},{8,4},{12,8},{16,12},{20,16},{24,20},{28,24},{32,28},{36,32}... | collective-permute-start | bytes 786440 | tf_op jit(solution)/shard_map/ppermute | solution.py:324
  346.1 15.4 %all-to-all-start.7 = ((bf16[4,256,256]{2,1,0:T(8,128)(2,1)}), bf16[4,256,256]{2,1,0:T(8,128)(2,1)S(1)}, u32[]{:S(2)}, u32[]{:S(2)}) async-start(bf16[4,256,256]{2,1,0:T(8,128)(2,1)} %shard_map.220), calls=%async_computation.7 | async-start | bytes 1048576 | tf_op jit(solution)/shard_map/all_to_all | solution.py:317
Sparse Core Ops, SparseCore 0:
  59.0 89.0 all-gather.2
where the time goes:
time: 371 us; the launch traced here: 370 us
  blocking collectives  154 us (42%)
  waiting for transfers between devices  82.6 us (22%)
  starting transfers between devices  79.3 us (21%)
  Pallas kernels  33.1 us (9%)
  between operations  14.4 us (4%)
  local copies, waits for them, and re-layouts  5.79 us (2%)
    all_to_all x2, blocking collectives, over_plane(): return lax.all_to_all(x, ('y', 'x'), 0, 0, tiled=True)  64.2 us
    ppermute x6, waiting for transfers between devices, halo(): return (lax.ppermute(last, NODES, up), lax.ppermute(first, NODES, down))  54.7 us
    all_to_all x1, blocking collectives, over_z(): arrived = lax.all_to_all(tiles, ('zh', 'heads'), 0, 0, tiled=True)  49 us
    all_to_all x4, blocking collectives, exchange(): return lax.all_to_all(x, 'heads', 0, 0, tiled=True)  41.1 us
    ppermute x3, starting transfers between devices, over_cores(): return lax.ppermute(x, 'core', [(0, 1), (1, 0)])  27.6 us
    ppermute x6, starting transfers between devices, trade(): out.append(lax.ppermute(parts[k], 'heads', [(i, i ^ k) for i in range(4)]))  23.2 us
    ppermute x6, starting transfers between devices, halo(): return (lax.ppermute(last, NODES, up), lax.ppermute(first, NODES, down))  18.9 us
    ppermute x6, waiting for transfers between devices, trade(): out.append(lax.ppermute(parts[k], 'heads', [(i, i ^ k) for i in range(4)]))  17.5 us
  transfers between devices with their start and end apart: 18, of which 9 were waited for; matrix products, arithmetic and copies ran while one was open for 0% of the time, Pallas kernels for 6%

commit v1 on v0

--- a/solution.py
+++ b/solution.py
@@ -65,27 +65,48 @@
 
 
 def pack_kernel(*refs):
-    *sources, out = refs
+    *sources, near, far = refs
     t = 0
     for source in sources:
         whole = source[...]
         for k in range(0, whole.shape[1], 128):
-            for g in range(out.shape[0]):
-                out[g, t] = whole[:, k : k + 128]
+            tile = whole[:, k : k + 128]
+            if t < near.shape[1]:
+                for g in range(near.shape[0]):
+                    near[g, t] = tile
+            else:
+                far[t - near.shape[1]] = tile
             t += 1
 
 
-def regroup_kernel(counts, src, *outs):
-    first = 0
-    for out, members in zip(outs, counts):
-        column = 0
-        for count in members:
-            for h in range(4):
+def regroup_near_kernel(src, out):
+    for t in range(src.shape[2]):
+        for h in range(4):
+            for z in range(4):
+                tile = src[h, z, t]
+                column = (4 * t + h) * 128
+                for g in range(out.shape[0]):
+                    out[g, z, :, column : column + 128] = tile
+
+
+def stack_kernel(pos, x0, x1, x2, x3, out):
+    for k, part in enumerate((x0, x1, x2, x3)):
+        out[(pos[4] + 4 - k) % 4] = part[...]
+
+
+def regroup_far_kernel(counts, pos, x0, x1, x2, x3, *outs):
+    for n, part in enumerate((x0, x1, x2, x3)):
+        h = pos[2] ^ n
+        first = 0
+        for out, members in zip(outs, counts):
+            column = 0
+            for count in members:
                 for k in range(count):
+                    at = pl.multiple_of((column + h * count + k) * 128, 128)
                     for z in range(4):
-                        out[z, :, column : column + 128] = src[z * 4 + h, first + k]
-                    column += 128
-            first += count
+                        out[z, :, pl.ds(at, 128)] = part[z, first + k]
+                first += count
+                column += 4 * count
 
 
 class Chunk:
@@ -273,16 +294,19 @@
         kv[g, :, 512:] = values
 
 
-def decode_kernel(pos, blocks, count, grid, own, before, after, mine, theirs, out, wq, wo, tiles,
-                  picked, sems):
-    weights = Weights(CHUNK_C, (4, 5), pos, mine, theirs, (wq, wo), sems)
+def queries_kernel(pos, grid, mine, theirs, out, wq, sems):
+    weights = Weights(CHUNK_C, (4,), pos, mine, theirs, (wq,), sems)
+    out[...] = (mm(normalize(wide(grid)), weights.get(0)) * SCALE).astype(BF16)
+
+
+def decode_kernel(pos, blocks, count, grid, queries, own, before, after, mine, theirs, out, wo,
+                  tiles, picked, sems):
+    weights = Weights(CHUNK_C, (5,), pos, mine, theirs, (wo,), sems)
     tiles[0] = before[...]
     for j in range(4):
         half = slice((j % 2) * 64, (j % 2) * 64 + 64)
         tiles[1 + j // 2, half] = own[j]
     tiles[3] = after[...]
-    grid_rows = wide(grid)
-    queries = (mm(normalize(grid_rows), weights.get(0)) * SCALE).astype(BF16)
     start = pos[0] * 2 - 1
     slots = blocks.shape[1]
     column = lax.broadcasted_iota(jnp.int32, (TILE, slots * TILE), 1)
@@ -308,7 +332,7 @@
             )
         )
     decoded = jnp.concatenate(mixtures, axis=0)
-    result = (grid_rows.astype(F32) + mm_t(decoded, weights.get(1))).astype(BF16)
+    result = (wide(grid).astype(F32) + mm_t(decoded, weights.get(0))).astype(BF16)
     for j in range(4):
         out[j] = result[:, j * 256 : (j + 1) * 256]
 
@@ -344,11 +368,9 @@
 
 
 def pack(sources):
-    width = sum(w.shape[1] // 128 for w in sources)
-    (tiles,) = call(
-        pack_kernel, [(16, width, 8, 128)], [in_vmem()] * len(sources), room=56
+    return call(
+        pack_kernel, [(4, 3, 8, 128), (17, 8, 128)], [in_vmem()] * len(sources), room=56
     )(*sources)
-    return tiles
 
 
 def to_everyone(x):
@@ -357,15 +379,6 @@
 
 def over_plane(x):
     return lax.all_to_all(x, ("y", "x"), 0, 0, tiled=True)
-
-
-def over_z(tiles, counts):
-    arrived = lax.all_to_all(tiles, ("zh", "heads"), 0, 0, tiled=True)
-    return call(
-        functools.partial(regroup_kernel, counts),
-        [(4, 8, 4 * sum(count) * 128) for count in counts],
-        [in_vmem()],
-    )(arrived)
 
 
 def local(
@@ -394,21 +407,36 @@
     position = lax.axis_index(NODES)
     mesh_tiles = lax.axis_size(NODES) * 2
     pos = jnp.stack(
-        [position, lax.axis_index("core"), lax.axis_index("heads"), jnp.int32(mesh_tiles)]
+        [position, lax.axis_index("core"), lax.axis_index("heads"), jnp.int32(mesh_tiles),
+         lax.axis_index("zh")]
     ).astype(jnp.int32)
 
-    counts = ((1, 1, 1), (1, 1, 1, 1, 1), (4, 4, 1, 1, 1, 1))
-    tiles = pack(
+    counts = ((1, 1, 1, 1, 1), (4, 4, 1, 1, 1, 1))
+    near, far = pack(
         (
             encoder_key, encoder_value, encoder_query, encoder_output.T, window_query, window_key,
             window_value, window_output.T, expand_weight, shrink_weight.T, decoder_key,
             decoder_value, decoder_query, decoder_output.T,
         )
     )
-    rows_a, rows_b, rows_c = over_z(tiles, counts)
-    copies_a = to_everyone(rows_a)
+    near = lax.all_to_all(near, "zh", 0, 0, tiled=True)
+    near = exchange(jnp.broadcast_to(near[None], (4, *near.shape)))
+    (copies_a,) = call(regroup_near_kernel, [(16, 4, 8, 1536)], [in_vmem()], room=8)(near)
     mine_a = over_plane(copies_a)
     theirs_a = over_cores(mine_a)
+    mine_a, theirs_a = in_hbm(mine_a), in_hbm(theirs_a)
+
+    far = [after_it(far, copies_a)] * 4
+    far = [far[0]] + [
+        lax.ppermute(far[k], "zh", [(i, (i + k) % 4) for i in range(4)]) for k in range(1, 4)
+    ]
+    (far,) = call(stack_kernel, [(4, 17, 8, 128)], [in_smem()] + [in_vmem()] * 4, room=4)(pos, *far)
+    rows_b, rows_c = call(
+        functools.partial(regroup_far_kernel, counts),
+        [(4, 8, 2560), (4, 8, 6144)],
+        [in_smem()] + [in_vmem()] * 4,
+        room=8,
+    )(pos, *trade([far] * 4))
     mine_c = lax.all_gather(rows_c, ("y", "x"))
 
     head = lax.axis_index("heads")
@@ -475,17 +503,24 @@
         room=24,
     )(pos, windowed, kept, mine_b, theirs_b, mine_c, theirs_c)
     own = exchange(spread)
+    before, after = halo(own[2:].reshape(TILE, D), own[:2].reshape(TILE, D))
     mesh_out = exchange(sent).reshape(256, 256)
-    before, after = halo(own[2:].reshape(TILE, D), own[:2].reshape(TILE, D))
-    pair = weight_scratch(CHUNK_C, (4, 5))
+    (queries,) = call(
+        queries_kernel,
+        [(256, 512)],
+        [in_smem(), in_vmem()] + [in_any()] * 2,
+        weight_scratch(CHUNK_C, (4,)),
+        room=12,
+    )(pos, grid, mine_c, theirs_c)
+    last = weight_scratch(CHUNK_C, (5,))
     (sent,) = call(
         decode_kernel,
         [(4, 256, 256)],
-        [in_smem()] * 3 + [in_vmem()] * 4 + [in_any()] * 2,
-        pair[:-1]
-        + [pltpu.VMEM((4, TILE, D), BF16), pltpu.VMEM((3 * TILE, D), BF16), pair[-1]],
-        room=20,
-    )(pos, decoder_blocks, decoder_count, grid, own, before, after, mine_c, theirs_c)
+        [in_smem()] * 3 + [in_vmem()] * 5 + [in_any()] * 2,
+        last[:-1]
+        + [pltpu.VMEM((4, TILE, D), BF16), pltpu.VMEM((3 * TILE, D), BF16), last[-1]],
+        room=16,
+    )(pos, decoder_blocks, decoder_count, grid, queries, own, before, after, mine_c, theirs_c)
     grid_out = exchange(sent).reshape(1024, 256)
     return grid_out, mesh_out
 

time: 371 us -> 367 us (0.989)
  blocking collectives: 154 us -> 134 us
  starting transfers between devices: 79.3 us -> 87.9 us
  waiting for transfers between devices: 82.6 us -> 87.8 us
    all_to_all x1, blocking collectives: 49 us -> 26.3 us  [local(): near = lax.all_to_all(near, 'zh', 0, 0, tiled=True)]
    all_to_all x4 -> x5, blocking collectives: 41.1 us -> 55.3 us  [exchange(): return lax.all_to_all(x, 'heads', 0, 0, tiled=True)]
    ppermute x3, starting transfers between devices: 27.6 us -> 14.8 us  [over_cores(): return lax.ppermute(x, 'core', [(0, 1), (1, 0)])]
    all_to_all x2, blocking collectives: 64.2 us -> 52.3 us  [over_plane(): return lax.all_to_all(x, ('y', 'x'), 0, 0, tiled=True)]
    ppermute x0 -> x3, starting transfers between devices: none -> 11.5 us  [local(): lax.ppermute(far[k], 'zh', [(i, (i + k) % 4) for i in range(4)])]
    ppermute x0 -> x3, waiting for transfers between devices: none -> 7.84 us  [local(): lax.ppermute(far[k], 'zh', [(i, (i + k) % 4) for i in range(4)])]
    ppermute x6, waiting for transfers between devices: 54.7 us -> 48.4 us  [halo(): return (lax.ppermute(last, NODES, up), lax.ppermute(first, NODES, down))]
    ppermute x6, starting transfers between devices: 18.9 us -> 24.8 us  [halo(): return (lax.ppermute(last, NODES, up), lax.ppermute(first, NODES, down))]
  transfers between devices with their start and end apart: 18 -> 24, of which waited for: 9 -> 12; matrix products, arithmetic and copies ran while one was open for 0% -> 0% of each run, Pallas kernels for 6% -> 6%
where the time goes in v1:
time: 367 us; the launch traced here: 366 us
  blocking collectives  134 us (37%)
  starting transfers between devices  87.9 us (24%)
  waiting for transfers between devices  87.8 us (24%)
  Pallas kernels  35.9 us (10%)
  between operations  14.5 us (4%)
  local copies, waits for them, and re-layouts  5.46 us (1%)
    all_to_all x5, blocking collectives, exchange(): return lax.all_to_all(x, 'heads', 0, 0, tiled=True)  55.3 us
    all_to_all x2, blocking collectives, over_plane(): return lax.all_to_all(x, ('y', 'x'), 0, 0, tiled=True)  52.3 us
    ppermute x6, waiting for transfers between devices, halo(): return (lax.ppermute(last, NODES, up), lax.ppermute(first, NODES, down))  48.4 us
    ppermute x9, starting transfers between devices, trade(): out.append(lax.ppermute(parts[k], 'heads', [(i, i ^ k) for i in range(4)]))  28.2 us
    all_to_all x1, blocking collectives, local(): near = lax.all_to_all(near, 'zh', 0, 0, tiled=True)  26.3 us
    ppermute x6, starting transfers between devices, halo(): return (lax.ppermute(last, NODES, up), lax.ppermute(first, NODES, down))  24.8 us
    ppermute x9, waiting for transfers between devices, trade(): out.append(lax.ppermute(parts[k], 'heads', [(i, i ^ k) for i in range(4)]))  21.2 us
    ppermute x3, starting transfers between devices, over_cores(): return lax.ppermute(x, 'core', [(0, 1), (1, 0)])  14.8 us
  transfers between devices with their start and end apart: 24, of which 12 were waited for; matrix products, arithmetic and copies ran while one was open for 0% of the time, Pallas kernels for 6%

profile of v1, /device:TPU:31, one launch (start us, length us, event | category | flops | bytes accessed | tf_op | source)
XLA Modules:
  0.0 365.5 jit_solution(15466150804561083625)
XLA Ops:
  8.7 26.3 %all_to_all.50 = bf16[4,3,8,128]{3,2,1,0:T(8,128)(2,1)S(1)} all-to-all(bf16[4,3,8,128]{3,2,1,0:T(8,128)(2,1)} %get-tuple-element.24), channel_id=1, replica_groups=mesh['zh'=4,'y'=4,'x'=4,'core'=2,'heads'=4] {'zh'}, dimensions={0} | all-to-all | bytes 49152 | tf_op jit(solution)/shard_map/all_to_all | solution.py:422
  35.0 7.6 %all_to_all.51.src = bf16[4,4,3,8,128]{4,3,2,1,0:T(8,128)(2,1)S(1)} all-to-all(bf16[4,4,3,8,128]{4,3,2,1,0:T(8,128)(2,1)S(1)} %broadcast_in_dim.4), channel_id=1, replica_groups=mesh['zh'=4,'y'=4,'x'=4,'core'=2,'heads'=4] {'heads'}, dimensions={0} | all-to-all | bytes 196608 | tf_op jit(solution)/shard_map/all_to_all | solution.py:341
  42.9 2.2 collective-permute-start.4
  45.1 7.0 %collective-permute-start.5 = (bf16[17,8,128]{2,1,0:T(8,128)(2,1)}, bf16[17,8,128]{2,1,0:T(8,128)(2,1)S(1)}, u32[]{:S(2)}, u32[]{:S(2)}) collective-permute-start(bf16[17,8,128]{2,1,0:T(8,128)(2,1)} %get-tuple-element.29.x0), channel_id=1, source_target_pairs={{0,256},{128,384},{256,0},{384,128},{1,257},{129,385},{257,1},{385... | collective-permute-start | bytes 104456 | tf_op jit(solution)/shard_map/ppermute | solution.py:431
  52.1 2.3 collective-permute-start.6
  54.5 4.2 %collective-permute-done.5.x2 = bf16[17,8,128]{2,1,0:T(8,128)(2,1)S(1)} collective-permute-done((bf16[17,8,128]{2,1,0:T(8,128)(2,1)}, bf16[17,8,128]{2,1,0:T(8,128)(2,1)S(1)}, u32[]{:S(2)}, u32[]{:S(2)}) %collective-permute-start.5) | collective-permute-done | bytes 34848 | tf_op jit(solution)/shard_map/ppermute | solution.py:431
  58.7 3.6 collective-permute-done.6.x3
  63.7 2.1 collective-permute-start.7
  65.8 1.9 collective-permute-start.8
  67.7 5.2 %collective-permute-start.9 = (bf16[4,17,8,128]{3,2,1,0:T(8,128)(2,1)S(1)}, bf16[4,17,8,128]{3,2,1,0:T(8,128)(2,1)S(1)}, u32[]{:S(2)}, u32[]{:S(2)}) collective-permute-start(bf16[4,17,8,128]{3,2,1,0:T(8,128)(2,1)S(1)} %shard_map.215.x0), channel_id=1, source_target_pairs={{0,3},{1,2},{2,1},{3,0},{4,7},{5,6},{6,5},{7,4},{8,11},{9,10},{10,... | collective-permute-start | bytes 417800 | tf_op jit(solution)/shard_map/ppermute | solution.py:366
  73.9 2.6 collective-permute-done.9.x3
  77.9 19.4 %all_to_all.52.mine = bf16[16,4,8,1536]{3,2,1,0:T(8,128)(2,1)} all-to-all(bf16[16,4,8,1536]{3,2,1,0:T(8,128)(2,1)S(1)} %shard_map.213), channel_id=1, replica_groups=mesh['zh'=4,'y'=4,'x'=4,'core'=2,'heads'=4] {'y','x'}, dimensions={0} | all-to-all | bytes 3145728 | tf_op jit(solution)/shard_map/all_to_all | solution.py:381
  97.5 32.9 %all_to_all.53.mine.mine_b = bf16[16,4,8,2560]{3,2,1,0:T(8,128)(2,1)S(1)} all-to-all(bf16[16,4,8,2560]{3,2,1,0:T(8,128)(2,1)S(1)} %broadcast_in_dim.5), channel_id=1, replica_groups=mesh['zh'=4,'y'=4,'x'=4,'core'=2,'heads'=4] {'y','x'}, dimensions={0} | all-to-all | bytes 5242880 | tf_op jit(solution)/shard_map/all_to_all | solution.py:381
  130.4 10.9 %collective-permute-start.15 = (bf16[16,4,8,2560]{3,2,1,0:T(8,128)(2,1)S(1)}, bf16[16,4,8,2560]{3,2,1,0:T(8,128)(2,1)}, u32[]{:S(2)}, u32[]{:S(2)}) collective-permute-start(bf16[16,4,8,2560]{3,2,1,0:T(8,128)(2,1)S(1)} %all_to_all.53.mine.mine_b), channel_id=1, source_target_pairs={{0,4},{4,0},{1,5},{5,1},{2,6},{6,2},{3,7},{7,3},{8,12},{12,8},{9,1... | collective-permute-start | bytes 7864328 | tf_op jit(solution)/shard_map/ppermute | solution.py:360
  141.4 1.9 collective-permute-start.3
  143.5 5.4 %collective-permute-start.2 = (bf16[320,256]{1,0:T(8,128)(2,1)S(1)}, bf16[320,256]{1,0:T(8,128)(2,1)S(1)}, u32[]{:S(2)}, u32[]{:S(2)}) collective-permute-start(bf16[320,256]{1,0:T(8,128)(2,1)S(1)} %pad_maximum_fusion.3), channel_id=1, source_target_pairs={{0,3},{1,2},{2,1},{3,0},{4,7},{5,6},{6,5},{7,4},{8,11},{9,10},{10,... | collective-permute-start | bytes 491528 | tf_op jit(solution)/shard_map/ppermute | solution.py:366
  148.9 2.0 collective-permute-start.1
  150.9 2.2 collective-permute-start
  153.2 10.9 %collective-permute-done.1.x2 = bf16[320,256]{1,0:T(8,128)(2,1)S(1)} collective-permute-done((bf16[320,256]{1,0:T(8,128)(2,1)S(1)}, bf16[320,256]{1,0:T(8,128)(2,1)S(1)}, u32[]{:S(2)}, u32[]{:S(2)}) %collective-permute-start.1) | collective-permute-done | bytes 163872 | tf_op jit(solution)/shard_map/ppermute | solution.py:366
  164.1 3.5 shard_map.214
  167.6 1.9 collective-permute-start.10
  169.5 2.6 collective-permute-start.11
  172.2 4.7 %collective-permute-start.12 = (bf16[288,256]{1,0:T(8,128)(2,1)S(1)}, bf16[288,256]{1,0:T(8,128)(2,1)S(1)}, u32[]{:S(2)}, u32[]{:S(2)}) collective-permute-start(bf16[288,256]{1,0:T(8,128)(2,1)S(1)} %get-tuple-element.34), channel_id=1, source_target_pairs={{0,3},{1,2},{2,1},{3,0},{4,7},{5,6},{6,5},{7,4},{8,11},{9,10},{10,... | collective-permute-start | bytes 442376 | tf_op jit(solution)/shard_map/ppermute | solution.py:366
  176.9 6.8 %collective-permute-done.11.x2 = bf16[288,256]{1,0:T(8,128)(2,1)S(1)} collective-permute-done((bf16[288,256]{1,0:T(8,128)(2,1)S(1)}, bf16[288,256]{1,0:T(8,128)(2,1)S(1)}, u32[]{:S(2)}, u32[]{:S(2)}) %collective-permute-start.11) | collective-permute-done | bytes 147488 | tf_op jit(solution)/shard_map/ppermute | solution.py:366
  184.3 11.3 %collective-permute-start.13 = (bf16[2,256,256]{2,1,0:T(8,128)(2,1)S(1)}, bf16[2,256,256]{2,1,0:T(8,128)(2,1)S(1)}, u32[]{:S(2)}, u32[]{:S(2)}) collective-permute-start(bf16[2,256,256]{2,1,0:T(8,128)(2,1)S(1)} %get-tuple-element.36), channel_id=1, source_target_pairs={{0,4},{4,8},{8,12},{12,16},{16,20},{20,24},{24,28},{28,32},{32,36}... | collective-permute-start | bytes 786440 | tf_op jit(solution)/shard_map/ppermute | solution.py:348
  195.7 1.9 collective-permute-start.14
  199.0 12.8 %collective-permute-done.14.after = bf16[2,256,256]{2,1,0:T(8,128)(2,1)S(1)} collective-permute-done((bf16[2,256,256]{2,1,0:T(8,128)(2,1)S(1)}, bf16[2,256,256]{2,1,0:T(8,128)(2,1)S(1)}, u32[]{:S(2)}, u32[]{:S(2)}) %collective-permute-start.14) | collective-permute-done | bytes 262176 | tf_op jit(solution)/shard_map/ppermute | solution.py:348
  211.8 2.6 shard_map.218
  214.5 16.1 %all_to_all.54.encoded = bf16[4,64,128]{2,1,0:T(8,128)(2,1)S(1)} all-to-all(bf16[4,64,128]{2,1,0:T(8,128)(2,1)S(1)} %shard_map.218), channel_id=1, replica_groups=mesh['zh'=4,'y'=4,'x'=4,'core'=2,'heads'=4] {'heads'}, dimensions={0} | all-to-all | bytes 131072 | tf_op jit(solution)/shard_map/all_to_all | solution.py:341
  230.6 3.7 %shard_map.219 = (bf16[4,64,384]{2,1,0:T(8,128)(2,1)S(1)}, bf16[64,1024]{1,0:T(8,128)(2,1)S(1)}) custom-call(s32[5]{0:T(128)S(1)} %stack.19.pos, bf16[4,64,128]{2,1,0:T(8,128)(2,1)S(1)} %all_to_all.54.encoded, bf16[4,64,256]{2,1,0:T(8,128)(2,1)S(1)} %get-tuple-element.38.mesh, bf16[16,4,8,2560]{3,2,1,0:T(8,128)(2,1)} %copy-done.6, ...), custom_call_target="tpu_custom_call" | custom-call | flops 268435456 | bytes 1048576 | tf_op jit(solution)/shard_map/pallas_call | solution.py:477
  234.3 8.0 %all_to_all.55.own = bf16[4,64,384]{2,1,0:T(8,128)(2,1)S(1)} all-to-all(bf16[4,64,384]{2,1,0:T(8,128)(2,1)S(1)} %get-tuple-element.41), channel_id=1, replica_groups=mesh['zh'=4,'y'=4,'x'=4,'core'=2,'heads'=4] {'heads'}, dimensions={0} | all-to-all | bytes 393216 | tf_op jit(solution)/shard_map/all_to_all | solution.py:341
  242.3 4.4 %collective-permute-start.16 = (bf16[4,64,256]{2,1,0:T(8,128)(2,1)S(1)}, bf16[4,64,256]{2,1,0:T(8,128)(2,1)S(1)}, u32[]{:S(2)}, u32[]{:S(2)}) collective-permute-start(bf16[4,64,256]{2,1,0:T(8,128)(2,1)S(1)} %slice.12), channel_id=1, source_target_pairs={{0,4},{4,8},{8,12},{12,16},{16,20},{20,24},{24,28},{28,32},{32,36}... | collective-permute-start | bytes 393224 | tf_op jit(solution)/shard_map/ppermute | solution.py:348
  246.7 1.9 collective-permute-start.17
  248.6 16.9 %collective-permute-done.17.after = bf16[4,64,256]{2,1,0:T(8,128)(2,1)S(1)} collective-permute-done((bf16[4,64,256]{2,1,0:T(8,128)(2,1)S(1)}, bf16[4,64,256]{2,1,0:T(8,128)(2,1)S(1)}, u32[]{:S(2)}, u32[]{:S(2)}) %collective-permute-start.17) | collective-permute-done | bytes 131104 | tf_op jit(solution)/shard_map/ppermute | solution.py:348
  265.5 1.9 collective-permute-start.18
  267.4 2.1 shard_map.221
  269.6 7.0 %all_to_all.56.windowed = bf16[4,64,128]{2,1,0:T(8,128)(2,1)S(1)} all-to-all(bf16[4,64,128]{2,1,0:T(8,128)(2,1)S(1)} %shard_map.221), channel_id=1, replica_groups=mesh['zh'=4,'y'=4,'x'=4,'core'=2,'heads'=4] {'heads'}, dimensions={0} | all-to-all | bytes 131072 | tf_op jit(solution)/shard_map/all_to_all | solution.py:341
  277.8 2.7 copy-done.5
  280.4 9.2 %shard_map.222 = (bf16[4,64,256]{2,1,0:T(8,128)(2,1)}, bf16[4,64,1024]{2,1,0:T(8,128)(2,1)S(1)}) custom-call(s32[5]{0:T(128)S(1)} %stack.19.pos, bf16[4,64,128]{2,1,0:T(8,128)(2,1)S(1)} %all_to_all.56.windowed, bf16[64,1024]{1,0:T(8,128)(2,1)S(1)} %get-tuple-element.43.kept, bf16[16,4,8,2560]{3,2,1,0:T(8,128)(2,1)} %copy-done.6, ...), custom_call_target="tpu_custom_call" | custom-call | flops 268435456 | bytes 1048576 | tf_op jit(solution)/shard_map/pallas_call | solution.py:498
  289.7 16.6 %all_to_all.57.own = bf16[4,64,1024]{2,1,0:T(8,128)(2,1)S(1)} all-to-all(bf16[4,64,1024]{2,1,0:T(8,128)(2,1)S(1)} %get-tuple-element.44), channel_id=1, replica_groups=mesh['zh'=4,'y'=4,'x'=4,'core'=2,'heads'=4] {'heads'}, dimensions={0} | all-to-all | bytes 1048576 | tf_op jit(solution)/shard_map/all_to_all | solution.py:341
  306.3 3.3 all-to-all-start.9
  309.6 2.5 collective-permute-start.19
  312.1 2.8 collective-permute-start.20
  315.0 2.4 shard_map.220.queries
  317.4 17.3 %collective-permute-done.20.after = bf16[128,1024]{1,0:T(8,128)(2,1)S(1)} collective-permute-done((bf16[128,1024]{1,0:T(8,128)(2,1)S(1)}, bf16[128,1024]{1,0:T(8,128)(2,1)S(1)}, u32[]{:S(2)}, u32[]{:S(2)}) %collective-permute-start.20) | collective-permute-done | bytes 262176 | tf_op jit(solution)/shard_map/ppermute | solution.py:348
  334.7 8.0 %shard_map.223 = bf16[4,256,256]{2,1,0:T(8,128)(2,1)} custom-call(s32[5]{0:T(128)S(1)} %stack.19.pos, s32[8,3]{1,0:T(8,128)S(1)} %copy.24.blocks, s32[8]{0:T(128)S(1)} %copy-done.2, bf16[4,256,256]{2,1,0:T(8,128)(2,1)S(1)} %get-tuple-element.27.grid, bf16[256,512]{1,0:T(8,128)(2,1)S(1)} %shard_map.220.queries, bf16[4,64,1024]{2,1,0:T(8,128)(2,1)S(1)} %all_to_all.57.own, ...), custom_call_target="tpu_custom_call" | custom-call | flops 268435456 | bytes 1048576 | tf_op jit(solution)/shard_map/pallas_call | solution.py:516
  342.8 5.3 %all-to-all-start.8 = ((bf16[4,256,256]{2,1,0:T(8,128)(2,1)}), bf16[4,256,256]{2,1,0:T(8,128)(2,1)S(1)}, u32[]{:S(2)}, u32[]{:S(2)}) async-start(bf16[4,256,256]{2,1,0:T(8,128)(2,1)} %shard_map.223), calls=%async_computation.8 | async-start | bytes 1048576 | tf_op jit(solution)/shard_map/all_to_all | solution.py:341
  348.1 9.1 %all-to-all-done.8 = bf16[4,256,256]{2,1,0:T(8,128)(2,1)S(1)} async-done(((bf16[4,256,256]{2,1,0:T(8,128)(2,1)}), bf16[4,256,256]{2,1,0:T(8,128)(2,1)S(1)}, u32[]{:S(2)}, u32[]{:S(2)}) %all-to-all-start.8) | async-done | bytes 524320 | tf_op jit(solution)/shard_map/all_to_all | solution.py:341
  (55 shorter events, 10.8 us)
Async XLA Ops:
  7.2 258.3 %all-gather.3.cloned.1.call-start = ((), (), s32[]{:S(2)}) async-start(), calls=%async_computation.10 | async-start | bytes 6684672 | tf_op jit(solution)/shard_map/all_gather | solution.py:440
  42.9 11.6 %collective-permute-start.4 = (bf16[17,8,128]{2,1,0:T(8,128)(2,1)}, bf16[17,8,128]{2,1,0:T(8,128)(2,1)S(1)}, u32[]{:S(2)}, u32[]{:S(2)}) collective-permute-start(bf16[17,8,128]{2,1,0:T(8,128)(2,1)} %get-tuple-element.29.x0), channel_id=1, source_target_pairs={{0,128},{128,256},{256,384},{384,0},{1,129},{129,257},{257,385},{3... | collective-permute-start | bytes 104456 | tf_op jit(solution)/shard_map/ppermute | solution.py:431
  45.1 13.6 %collective-permute-start.5 = (bf16[17,8,128]{2,1,0:T(8,128)(2,1)}, bf16[17,8,128]{2,1,0:T(8,128)(2,1)S(1)}, u32[]{:S(2)}, u32[]{:S(2)}) collective-permute-start(bf16[17,8,128]{2,1,0:T(8,128)(2,1)} %get-tuple-element.29.x0), channel_id=1, source_target_pairs={{0,256},{128,384},{256,0},{384,128},{1,257},{129,385},{257,1},{385... | collective-permute-start | bytes 104456 | tf_op jit(solution)/shard_map/ppermute | solution.py:431
  52.1 10.2 %collective-permute-start.6 = (bf16[17,8,128]{2,1,0:T(8,128)(2,1)}, bf16[17,8,128]{2,1,0:T(8,128)(2,1)S(1)}, u32[]{:S(2)}, u32[]{:S(2)}) collective-permute-start(bf16[17,8,128]{2,1,0:T(8,128)(2,1)} %get-tuple-element.29.x0), channel_id=1, source_target_pairs={{0,384},{128,0},{256,128},{384,256},{1,385},{129,1},{257,129},{385... | collective-permute-start | bytes 104456 | tf_op jit(solution)/shard_map/ppermute | solution.py:431
  62.3 0.8 copy-start.3
  63.7 9.3 %collective-permute-start.7 = (bf16[4,17,8,128]{3,2,1,0:T(8,128)(2,1)S(1)}, bf16[4,17,8,128]{3,2,1,0:T(8,128)(2,1)S(1)}, u32[]{:S(2)}, u32[]{:S(2)}) collective-permute-start(bf16[4,17,8,128]{3,2,1,0:T(8,128)(2,1)S(1)} %shard_map.215.x0), channel_id=1, source_target_pairs={{0,1},{1,0},{2,3},{3,2},{4,5},{5,4},{6,7},{7,6},{8,9},{9,8},{10,11... | collective-permute-start | bytes 417800 | tf_op jit(solution)/shard_map/ppermute | solution.py:366
  65.8 8.1 %collective-permute-start.8 = (bf16[4,17,8,128]{3,2,1,0:T(8,128)(2,1)S(1)}, bf16[4,17,8,128]{3,2,1,0:T(8,128)(2,1)S(1)}, u32[]{:S(2)}, u32[]{:S(2)}) collective-permute-start(bf16[4,17,8,128]{3,2,1,0:T(8,128)(2,1)S(1)} %shard_map.215.x0), channel_id=1, source_target_pairs={{0,2},{1,3},{2,0},{3,1},{4,6},{5,7},{6,4},{7,5},{8,10},{9,11},{10,... | collective-permute-start | bytes 417800 | tf_op jit(solution)/shard_map/ppermute | solution.py:366
  67.7 8.7 %collective-permute-start.9 = (bf16[4,17,8,128]{3,2,1,0:T(8,128)(2,1)S(1)}, bf16[4,17,8,128]{3,2,1,0:T(8,128)(2,1)S(1)}, u32[]{:S(2)}, u32[]{:S(2)}) collective-permute-start(bf16[4,17,8,128]{3,2,1,0:T(8,128)(2,1)S(1)} %shard_map.215.x0), channel_id=1, source_target_pairs={{0,3},{1,2},{2,1},{3,0},{4,7},{5,6},{6,5},{7,4},{8,11},{9,10},{10,... | collective-permute-start | bytes 417800 | tf_op jit(solution)/shard_map/ppermute | solution.py:366
  97.5 45.8 %copy-start.8 = (bf16[256,256]{1,0:T(8,128)(2,1)S(1)}, bf16[256,256]{1,0:T(8,128)(2,1)}, u32[]{:S(2)}) copy-start(bf16[256,256]{1,0:T(8,128)(2,1)} %param.22) | copy-start | bytes 393220
  97.5 45.8 %copy-start.7 = (bf16[1024,256]{1,0:T(8,128)(2,1)S(1)}, bf16[1024,256]{1,0:T(8,128)(2,1)}, u32[]{:S(2)}) copy-start(bf16[1024,256]{1,0:T(8,128)(2,1)} %param.21) | copy-start | bytes 1572868
  130.4 37.2 %copy-start.6 = (bf16[16,4,8,2560]{3,2,1,0:T(8,128)(2,1)}, bf16[16,4,8,2560]{3,2,1,0:T(8,128)(2,1)S(1)}, u32[]{:S(2)}) copy-start(bf16[16,4,8,2560]{3,2,1,0:T(8,128)(2,1)S(1)} %all_to_all.53.mine.mine_b) | copy-start | bytes 7864324
  130.4 100.2 %collective-permute-start.15 = (bf16[16,4,8,2560]{3,2,1,0:T(8,128)(2,1)S(1)}, bf16[16,4,8,2560]{3,2,1,0:T(8,128)(2,1)}, u32[]{:S(2)}, u32[]{:S(2)}) collective-permute-start(bf16[16,4,8,2560]{3,2,1,0:T(8,128)(2,1)S(1)} %all_to_all.53.mine.mine_b), channel_id=1, source_target_pairs={{0,4},{4,0},{1,5},{5,1},{2,6},{6,2},{3,7},{7,3},{8,12},{12,8},{9,1... | collective-permute-start | bytes 7864328 | tf_op jit(solution)/shard_map/ppermute | solution.py:360
  141.4 22.7 %collective-permute-start.3 = (bf16[16,4,8,1536]{3,2,1,0:T(8,128)(2,1)}, bf16[16,4,8,1536]{3,2,1,0:T(8,128)(2,1)}, u32[]{:S(2)}, u32[]{:S(2)}) collective-permute-start(bf16[16,4,8,1536]{3,2,1,0:T(8,128)(2,1)} %all_to_all.52.mine), channel_id=1, source_target_pairs={{0,4},{4,0},{1,5},{5,1},{2,6},{6,2},{3,7},{7,3},{8,12},{12,8},{9,1... | collective-permute-start | bytes 4718600 | tf_op jit(solution)/shard_map/ppermute | solution.py:360
  143.5 9.7 %collective-permute-start.2 = (bf16[320,256]{1,0:T(8,128)(2,1)S(1)}, bf16[320,256]{1,0:T(8,128)(2,1)S(1)}, u32[]{:S(2)}, u32[]{:S(2)}) collective-permute-start(bf16[320,256]{1,0:T(8,128)(2,1)S(1)} %pad_maximum_fusion.3), channel_id=1, source_target_pairs={{0,3},{1,2},{2,1},{3,0},{4,7},{5,6},{6,5},{7,4},{8,11},{9,10},{10,... | collective-permute-start | bytes 491528 | tf_op jit(solution)/shard_map/ppermute | solution.py:366
  148.9 15.3 %collective-permute-start.1 = (bf16[320,256]{1,0:T(8,128)(2,1)S(1)}, bf16[320,256]{1,0:T(8,128)(2,1)S(1)}, u32[]{:S(2)}, u32[]{:S(2)}) collective-permute-start(bf16[320,256]{1,0:T(8,128)(2,1)S(1)} %pad_maximum_fusion.2), channel_id=1, source_target_pairs={{0,2},{1,3},{2,0},{3,1},{4,6},{5,7},{6,4},{7,5},{8,10},{9,11},{10,... | collective-permute-start | bytes 491528 | tf_op jit(solution)/shard_map/ppermute | solution.py:366
  150.9 60.9 %copy-start = (s32[2,8]{1,0:T(2,128)S(1)}, s32[2,8]{1,0:T(2,128)}, u32[]{:S(2)}) copy-start(s32[2,8]{1,0:T(2,128)} %blocks.2) | copy-start | bytes 196
  150.9 60.9 %copy-start.1 = (s32[2]{0:T(128)S(1)}, s32[2]{0:T(128)}, u32[]{:S(2)}) copy-start(s32[2]{0:T(128)} %count.2) | copy-start | bytes 28
  150.9 13.2 %collective-permute-start = (bf16[320,256]{1,0:T(8,128)(2,1)S(1)}, bf16[320,256]{1,0:T(8,128)(2,1)S(1)}, u32[]{:S(2)}, u32[]{:S(2)}) collective-permute-start(bf16[320,256]{1,0:T(8,128)(2,1)S(1)} %pad_maximum_fusion.1), channel_id=1, source_target_pairs={{0,1},{1,0},{2,3},{3,2},{4,5},{5,4},{6,7},{7,6},{8,9},{9,8},{10,11... | collective-permute-start | bytes 491528 | tf_op jit(solution)/shard_map/ppermute | solution.py:366
  167.6 9.3 %collective-permute-start.10 = (bf16[288,256]{1,0:T(8,128)(2,1)S(1)}, bf16[288,256]{1,0:T(8,128)(2,1)S(1)}, u32[]{:S(2)}, u32[]{:S(2)}) collective-permute-start(bf16[288,256]{1,0:T(8,128)(2,1)S(1)} %get-tuple-element.32), channel_id=1, source_target_pairs={{0,1},{1,0},{2,3},{3,2},{4,5},{5,4},{6,7},{7,6},{8,9},{9,8},{10,11... | collective-permute-start | bytes 442376 | tf_op jit(solution)/shard_map/ppermute | solution.py:366
  169.5 14.2 %collective-permute-start.11 = (bf16[288,256]{1,0:T(8,128)(2,1)S(1)}, bf16[288,256]{1,0:T(8,128)(2,1)S(1)}, u32[]{:S(2)}, u32[]{:S(2)}) collective-permute-start(bf16[288,256]{1,0:T(8,128)(2,1)S(1)} %get-tuple-element.33), channel_id=1, source_target_pairs={{0,2},{1,3},{2,0},{3,1},{4,6},{5,7},{6,4},{7,5},{8,10},{9,11},{10,... | collective-permute-start | bytes 442376 | tf_op jit(solution)/shard_map/ppermute | solution.py:366
  172.2 11.6 %collective-permute-start.12 = (bf16[288,256]{1,0:T(8,128)(2,1)S(1)}, bf16[288,256]{1,0:T(8,128)(2,1)S(1)}, u32[]{:S(2)}, u32[]{:S(2)}) collective-permute-start(bf16[288,256]{1,0:T(8,128)(2,1)S(1)} %get-tuple-element.34), channel_id=1, source_target_pairs={{0,3},{1,2},{2,1},{3,0},{4,7},{5,6},{6,5},{7,4},{8,11},{9,10},{10,... | collective-permute-start | bytes 442376 | tf_op jit(solution)/shard_map/ppermute | solution.py:366
  184.3 14.6 %collective-permute-start.13 = (bf16[2,256,256]{2,1,0:T(8,128)(2,1)S(1)}, bf16[2,256,256]{2,1,0:T(8,128)(2,1)S(1)}, u32[]{:S(2)}, u32[]{:S(2)}) collective-permute-start(bf16[2,256,256]{2,1,0:T(8,128)(2,1)S(1)} %get-tuple-element.36), channel_id=1, source_target_pairs={{0,4},{4,8},{8,12},{12,16},{16,20},{20,24},{24,28},{28,32},{32,36}... | collective-permute-start | bytes 786440 | tf_op jit(solution)/shard_map/ppermute | solution.py:348
  195.7 16.1 %collective-permute-start.14 = (bf16[2,256,256]{2,1,0:T(8,128)(2,1)S(1)}, bf16[2,256,256]{2,1,0:T(8,128)(2,1)S(1)}, u32[]{:S(2)}, u32[]{:S(2)}) collective-permute-start(bf16[2,256,256]{2,1,0:T(8,128)(2,1)S(1)} %get-tuple-element.37), channel_id=1, source_target_pairs={{4,0},{8,4},{12,8},{16,12},{20,16},{24,20},{28,24},{32,28},{36,32}... | collective-permute-start | bytes 786440 | tf_op jit(solution)/shard_map/ppermute | solution.py:348
  230.6 36.8 %copy-start.4 = (s32[2,4]{1,0:T(2,128)S(1)}, s32[2,4]{1,0:T(2,128)}, u32[]{:S(2)}) copy-start(s32[2,4]{1,0:T(2,128)} %offsets.1) | copy-start | bytes 100
  242.3 6.3 %collective-permute-start.16 = (bf16[4,64,256]{2,1,0:T(8,128)(2,1)S(1)}, bf16[4,64,256]{2,1,0:T(8,128)(2,1)S(1)}, u32[]{:S(2)}, u32[]{:S(2)}) collective-permute-start(bf16[4,64,256]{2,1,0:T(8,128)(2,1)S(1)} %slice.12), channel_id=1, source_target_pairs={{0,4},{4,8},{8,12},{12,16},{16,20},{20,24},{24,28},{28,32},{32,36}... | collective-permute-start | bytes 393224 | tf_op jit(solution)/shard_map/ppermute | solution.py:348
  246.7 18.8 %collective-permute-start.17 = (bf16[4,64,256]{2,1,0:T(8,128)(2,1)S(1)}, bf16[4,64,256]{2,1,0:T(8,128)(2,1)S(1)}, u32[]{:S(2)}, u32[]{:S(2)}) collective-permute-start(bf16[4,64,256]{2,1,0:T(8,128)(2,1)S(1)} %slice.12), channel_id=1, source_target_pairs={{4,0},{8,4},{12,8},{16,12},{20,16},{24,20},{28,24},{32,28},{36,32}... | collective-permute-start | bytes 393224 | tf_op jit(solution)/shard_map/ppermute | solution.py:348
  265.5 12.3 %collective-permute-start.18 = (bf16[16,4,8,6144]{3,2,1,0:T(8,128)(2,1)}, bf16[16,4,8,6144]{3,2,1,0:T(8,128)(2,1)S(1)}, u32[]{:S(2)}, u32[]{:S(2)}) collective-permute-start(bf16[16,4,8,6144]{3,2,1,0:T(8,128)(2,1)} %bitcast.31), channel_id=1, source_target_pairs={{0,4},{4,0},{1,5},{5,1},{2,6},{6,2},{3,7},{7,3},{8,12},{12,8},{9,1... | collective-permute-start | bytes 18874376 | tf_op jit(solution)/shard_map/ppermute | solution.py:360
  277.8 2.7 copy-start.5
  280.4 34.5 %copy-start.9 = (s32[8,3]{0,1:T(4,128)S(1)}, s32[8,3]{0,1:T(4,128)}, u32[]{:S(2)}) copy-start(s32[8,3]{0,1:T(4,128)} %param.40) | copy-start | bytes 292
  306.3 36.5 %all-to-all-start.9 = ((bf16[4,64,256]{2,1,0:T(8,128)(2,1)}), bf16[4,64,256]{2,1,0:T(8,128)(2,1)S(1)}, u32[]{:S(2)}, u32[]{:S(2)}) async-start(bf16[4,64,256]{2,1,0:T(8,128)(2,1)} %get-tuple-element.45), calls=%async_computation.9 | async-start | bytes 262144 | tf_op jit(solution)/shard_map/all_to_all | solution.py:341
  309.6 7.8 %collective-permute-start.19 = (bf16[128,1024]{1,0:T(8,128)(2,1)S(1)}, bf16[128,1024]{1,0:T(8,128)(2,1)S(1)}, u32[]{:S(2)}, u32[]{:S(2)}) collective-permute-start(bf16[128,1024]{1,0:T(8,128)(2,1)S(1)} %bitcast.39), channel_id=1, source_target_pairs={{0,4},{4,8},{8,12},{12,16},{16,20},{20,24},{24,28},{28,32},{32,36}... | collective-permute-start | bytes 786440 | tf_op jit(solution)/shard_map/ppermute | solution.py:348
  312.1 22.6 %collective-permute-start.20 = (bf16[128,1024]{1,0:T(8,128)(2,1)S(1)}, bf16[128,1024]{1,0:T(8,128)(2,1)S(1)}, u32[]{:S(2)}, u32[]{:S(2)}) collective-permute-start(bf16[128,1024]{1,0:T(8,128)(2,1)S(1)} %bitcast.38), channel_id=1, source_target_pairs={{4,0},{8,4},{12,8},{16,12},{20,16},{24,20},{28,24},{32,28},{36,32}... | collective-permute-start | bytes 786440 | tf_op jit(solution)/shard_map/ppermute | solution.py:348
  315.0 19.7 %copy-start.2 = (s32[8]{0:T(128)S(1)}, s32[8]{0:T(128)}, u32[]{:S(2)}) copy-start(s32[8]{0:T(128)} %count.3) | copy-start | bytes 100
  342.8 14.5 %all-to-all-start.8 = ((bf16[4,256,256]{2,1,0:T(8,128)(2,1)}), bf16[4,256,256]{2,1,0:T(8,128)(2,1)S(1)}, u32[]{:S(2)}, u32[]{:S(2)}) async-start(bf16[4,256,256]{2,1,0:T(8,128)(2,1)} %shard_map.223), calls=%async_computation.8 | async-start | bytes 1048576 | tf_op jit(solution)/shard_map/all_to_all | solution.py:341
Sparse Core Ops, SparseCore 0:
  78.0 98.7 all-gather.2

commit v2 on v0

--- a/solution.py
+++ b/solution.py
@@ -75,17 +75,28 @@
             t += 1
 
 
-def regroup_kernel(counts, src, *outs):
+def regroup_kernel(counts, src, near, far):
     first = 0
-    for out, members in zip(outs, counts):
+    for out, members in zip((near, far), counts):
         column = 0
         for count in members:
             for h in range(4):
                 for k in range(count):
                     for z in range(4):
-                        out[z, :, column : column + 128] = src[z * 4 + h, first + k]
+                        tile = src[z * 4 + h, first + k]
+                        if out is near:
+                            for g in range(near.shape[0]):
+                                near[g, z, :, column : column + 128] = tile
+                        else:
+                            far[z, :, column : column + 128] = tile
                     column += 128
             first += count
+
+
+def own_kernel(pos, grid, mesh, out):
+    rows = grid.shape[1]
+    out[:rows, :] = grid[pos[2]]
+    out[rows:, :] = mesh[pos[2]]
 
 
 class Chunk:
@@ -111,8 +122,7 @@
 
 
 CHUNK_A = Chunk((512, 512, 512))
-CHUNK_B = Chunk((512, 512, 512, 512, 512))
-CHUNK_C = Chunk((2048, 2048, 512, 512, 512, 512))
+CHUNK_B = Chunk((512,) * 5 + (2048,) * 2 + (512,) * 4)
 
 
 def weight_scratch(chunk, members):
@@ -253,36 +263,37 @@
 
 
 def second_kernel(
-    pos, windowed, kept, mine_b, theirs_b, mine_c, theirs_c, mesh_out, kv, wo, up, down, wk, wv,
-    sems_b, sems_c
+    pos, windowed, kept, mine, theirs, mesh_out, kv, wo, up, down, wk, wv, sems
 ):
-    near = Weights(CHUNK_B, (4,), pos, mine_b, theirs_b, (wo,), sems_b)
-    far = Weights(CHUNK_C, (0, 1, 2, 3), pos, mine_c, theirs_c, (up, down, wk, wv), sems_c)
-    update = mm_t(wide(windowed), near.get(0))
+    weights = Weights(CHUNK_B, (4, 5, 6, 7, 8), pos, mine, theirs, (wo, up, down, wk, wv), sems)
+    update = mm_t(wide(windowed), weights.get(0))
     mesh_two = (kept[...].astype(F32) + update).astype(BF16)
-    hidden = mm(normalize(mesh_two), far.get(0))
+    hidden = mm(normalize(mesh_two), weights.get(1))
     hidden = (0.5 * hidden * (1.0 + lax.erf(hidden * (2.0**-0.5)))).astype(BF16)
-    result = (mesh_two.astype(F32) + mm_t(hidden, far.get(1))).astype(BF16)
+    result = (mesh_two.astype(F32) + mm_t(hidden, weights.get(2))).astype(BF16)
     for j in range(4):
         mesh_out[j] = result[:, j * 256 : (j + 1) * 256]
     norm_three = normalize(result)
-    keys = mm(norm_three, far.get(2)).astype(BF16)
-    values = mm(norm_three, far.get(3)).astype(BF16)
+    keys = mm(norm_three, weights.get(3)).astype(BF16)
+    values = mm(norm_three, weights.get(4)).astype(BF16)
     for g in range(4):
         kv[g, :, :512] = keys
         kv[g, :, 512:] = values
 
 
-def decode_kernel(pos, blocks, count, grid, own, before, after, mine, theirs, out, wq, wo, tiles,
-                  picked, sems):
-    weights = Weights(CHUNK_C, (4, 5), pos, mine, theirs, (wq, wo), sems)
+def queries_kernel(pos, grid, mine, theirs, out, wq, sems):
+    weights = Weights(CHUNK_B, (9,), pos, mine, theirs, (wq,), sems)
+    out[...] = (mm(normalize(wide(grid)), weights.get(0)) * SCALE).astype(BF16)
+
+
+def decode_kernel(pos, blocks, count, grid, queries, own, before, after, mine, theirs, out, wo,
+                  tiles, picked, sems):
+    weights = Weights(CHUNK_B, (10,), pos, mine, theirs, (wo,), sems)
     tiles[0] = before[...]
     for j in range(4):
         half = slice((j % 2) * 64, (j % 2) * 64 + 64)
         tiles[1 + j // 2, half] = own[j]
     tiles[3] = after[...]
-    grid_rows = wide(grid)
-    queries = (mm(normalize(grid_rows), weights.get(0)) * SCALE).astype(BF16)
     start = pos[0] * 2 - 1
     slots = blocks.shape[1]
     column = lax.broadcasted_iota(jnp.int32, (TILE, slots * TILE), 1)
@@ -308,7 +319,7 @@
             )
         )
     decoded = jnp.concatenate(mixtures, axis=0)
-    result = (grid_rows.astype(F32) + mm_t(decoded, weights.get(1))).astype(BF16)
+    result = (wide(grid).astype(F32) + mm_t(decoded, weights.get(0))).astype(BF16)
     for j in range(4):
         out[j] = result[:, j * 256 : (j + 1) * 256]
 
@@ -344,28 +355,14 @@
 
 
 def pack(sources):
-    width = sum(w.shape[1] // 128 for w in sources)
     (tiles,) = call(
-        pack_kernel, [(16, width, 8, 128)], [in_vmem()] * len(sources), room=56
+        pack_kernel, [(16, 20, 8, 128)], [in_vmem()] * len(sources), room=56
     )(*sources)
     return tiles
 
 
-def to_everyone(x):
-    return jnp.broadcast_to(x[None], (16, *x.shape))
-
-
 def over_plane(x):
     return lax.all_to_all(x, ("y", "x"), 0, 0, tiled=True)
-
-
-def over_z(tiles, counts):
-    arrived = lax.all_to_all(tiles, ("zh", "heads"), 0, 0, tiled=True)
-    return call(
-        functools.partial(regroup_kernel, counts),
-        [(4, 8, 4 * sum(count) * 128) for count in counts],
-        [in_vmem()],
-    )(arrived)
 
 
 def local(
@@ -394,10 +391,11 @@
     position = lax.axis_index(NODES)
     mesh_tiles = lax.axis_size(NODES) * 2
     pos = jnp.stack(
-        [position, lax.axis_index("core"), lax.axis_index("heads"), jnp.int32(mesh_tiles)]
+        [position, lax.axis_index("core"), lax.axis_index("heads"), jnp.int32(mesh_tiles),
+         lax.axis_index("zh")]
     ).astype(jnp.int32)
 
-    counts = ((1, 1, 1), (1, 1, 1, 1, 1), (4, 4, 1, 1, 1, 1))
+    counts = ((1, 1, 1), (1, 1, 1, 1, 1, 4, 4, 1, 1, 1, 1))
     tiles = pack(
         (
             encoder_key, encoder_value, encoder_query, encoder_output.T, window_query, window_key,
@@ -405,22 +403,31 @@
             decoder_value, decoder_query, decoder_output.T,
         )
     )
-    rows_a, rows_b, rows_c = over_z(tiles, counts)
-    copies_a = to_everyone(rows_a)
+    tiles = lax.all_to_all(tiles, ("zh", "heads"), 0, 0, tiled=True)
+    copies_a, rows = call(
+        functools.partial(regroup_kernel, counts),
+        [(16, 4, 8, 1536), (4, 8, 8704)],
+        [in_vmem()],
+    )(tiles)
+    mine = lax.all_gather(rows, ("y", "x"))
     mine_a = over_plane(copies_a)
     theirs_a = over_cores(mine_a)
-    mine_c = lax.all_gather(rows_c, ("y", "x"))
+
 
     head = lax.axis_index("heads")
-    both = [
+    grid_parts, mesh_parts = grid_state.reshape(4, 256, 256), mesh_state.reshape(4, 64, 256)
+    both = call(
+        own_kernel, [(320, 256)], [in_smem(), in_vmem(), in_vmem()], room=8
+    )(pos, grid_parts, mesh_parts)
+    both += tuple(
         jnp.concatenate(
             [
-                lax.dynamic_index_in_dim(after_it(x, copies_a).reshape(4, -1, 256), head ^ k, 0, False)
-                for x in (grid_state, mesh_state)
+                lax.dynamic_index_in_dim(after_it(x, copies_a), head ^ k, 0, False)
+                for x in (grid_parts, mesh_parts)
             ]
         )
-        for k in range(4)
-    ]
+        for k in range(1, 4)
+    )
     *sent, grid, mesh = call(
         inputs_kernel,
         [(288, 256)] * 4 + [(4, 256, 256), (4, 64, 256)],
@@ -428,8 +435,6 @@
         [pltpu.VMEM((4, 288, 256), BF16)] + weight_scratch(CHUNK_A, (0, 1, 2)),
         room=16,
     )(pos, *trade(both), mine_a, theirs_a)
-    copies_b = to_everyone(after_it(rows_b, mine_a))
-    mine_b = over_plane(copies_b)
     own, last, first = call(
         arrange_kernel,
         [(4, 288, 256), (2, 256, 256), (2, 256, 256)],
@@ -437,8 +442,6 @@
         room=8,
     )(pos, *trade(sent))
     before, after = halo(last, first)
-    theirs_b = over_cores(mine_b)
-    mine_b, theirs_b = in_hbm(mine_b), in_hbm(theirs_b)
     (sent,) = call(
         encode_kernel,
         [(4, 64, 128)],
@@ -446,19 +449,20 @@
         [pltpu.VMEM((16, TILE, 256), BF16), pltpu.VMEM((8 * TILE, 256), BF16)],
     )(pos, encoder_blocks, encoder_count, own, before, after)
     encoded = exchange(sent)
+    mine = after_it(mine, encoded)
+    theirs_b = over_cores(mine[:, :, :, :2048])
+    theirs = over_cores(mine)
+    mine, late = in_hbm(mine), in_hbm(theirs)
     sent, kept = call(
         first_kernel,
         [(4, 64, 384), (64, D)],
         [in_smem(), in_vmem(), in_vmem(), in_any(), in_any()],
         weight_scratch(CHUNK_B, (0, 1, 2, 3)),
         room=16,
-    )(pos, encoded, mesh, mine_b, theirs_b)
+    )(pos, encoded, mesh, mine, theirs_b)
     own = exchange(sent)
     side = own[:, :, PAIR:]
     before, after = halo(side, side)
-    mine_c = after_it(mine_c, (before, after))
-    theirs_c = over_cores(mine_c)
-    mine_c, theirs_c = in_hbm(mine_c), in_hbm(theirs_c)
     (sent,) = call(
         window_kernel,
         [(4, 64, 128)],
@@ -466,26 +470,32 @@
         [pltpu.VMEM((6, TILE, 256), BF16), pltpu.VMEM((4 * TILE, 256), BF16)],
     )(pos, window_offsets, own, before, after)
     windowed = exchange(sent)
-    near, far = weight_scratch(CHUNK_B, (4,)), weight_scratch(CHUNK_C, (0, 1, 2, 3))
     sent, spread = call(
         second_kernel,
         [(4, 64, 256), (4, 64, D)],
-        [in_smem(), in_vmem(), in_vmem()] + [in_any()] * 4,
-        near[:-1] + far[:-1] + [near[-1], far[-1]],
+        [in_smem(), in_vmem(), in_vmem()] + [in_any()] * 2,
+        weight_scratch(CHUNK_B, (4, 5, 6, 7, 8)),
         room=24,
-    )(pos, windowed, kept, mine_b, theirs_b, mine_c, theirs_c)
+    )(pos, windowed, kept, mine, theirs)
     own = exchange(spread)
+    before, after = halo(own[2:].reshape(TILE, D), own[:2].reshape(TILE, D))
     mesh_out = exchange(sent).reshape(256, 256)
-    before, after = halo(own[2:].reshape(TILE, D), own[:2].reshape(TILE, D))
-    pair = weight_scratch(CHUNK_C, (4, 5))
+    (queries,) = call(
+        queries_kernel,
+        [(256, 512)],
+        [in_smem(), in_vmem()] + [in_any()] * 2,
+        weight_scratch(CHUNK_B, (9,)),
+        room=12,
+    )(pos, grid, mine, late)
+    last = weight_scratch(CHUNK_B, (10,))
     (sent,) = call(
         decode_kernel,
         [(4, 256, 256)],
-        [in_smem()] * 3 + [in_vmem()] * 4 + [in_any()] * 2,
-        pair[:-1]
-        + [pltpu.VMEM((4, TILE, D), BF16), pltpu.VMEM((3 * TILE, D), BF16), pair[-1]],
-        room=20,
-    )(pos, decoder_blocks, decoder_count, grid, own, before, after, mine_c, theirs_c)
+        [in_smem()] * 3 + [in_vmem()] * 5 + [in_any()] * 2,
+        last[:-1]
+        + [pltpu.VMEM((4, TILE, D), BF16), pltpu.VMEM((3 * TILE, D), BF16), last[-1]],
+        room=16,
+    )(pos, decoder_blocks, decoder_count, grid, queries, own, before, after, mine, late)
     grid_out = exchange(sent).reshape(1024, 256)
     return grid_out, mesh_out
 

time: 371 us -> 345 us (0.930)
  blocking collectives: 154 us -> 115 us
  starting transfers between devices: 79.3 us -> 93.7 us
  waiting for transfers between devices: 82.6 us -> 75.1 us
    all_to_all x2 -> x1, blocking collectives: 64.2 us -> 26.4 us  [over_plane(): return lax.all_to_all(x, ('y', 'x'), 0, 0, tiled=True)]
    ppermute x6, starting transfers between devices: 18.9 us -> 42 us  [halo(): return (lax.ppermute(last, NODES, up), lax.ppermute(first, NODES, down))]
    ppermute x6, waiting for transfers between devices: 54.7 us -> 37.5 us  [halo(): return (lax.ppermute(last, NODES, up), lax.ppermute(first, NODES, down))]
    ppermute x3, starting transfers between devices: 27.6 us -> 15.2 us  [over_cores(): return lax.ppermute(x, 'core', [(0, 1), (1, 0)])]
    ppermute x3, waiting for transfers between devices: 1.24 us -> 12.9 us  [over_cores(): return lax.ppermute(x, 'core', [(0, 1), (1, 0)])]
    all_to_all x2, starting transfers between devices: 9.54 us -> 14.1 us  [exchange(): return lax.all_to_all(x, 'heads', 0, 0, tiled=True)]
    pallas_call x3 -> x5, Pallas kernels: 11.9 us -> 13.9 us  [the longest x1 8 us: local(): call(decode_kernel, [(4, 256, 256)], [in_smem()] * 3 + [in_vmem()] * 5 +...]
  transfers between devices with their start and end apart: 18 -> 18, of which waited for: 9 -> 8; matrix products, arithmetic and copies ran while one was open for 0% -> 1% of each run, Pallas kernels for 6% -> 7%
where the time goes in v2:
time: 345 us; the launch traced here: 344 us
  blocking collectives  115 us (33%)
  starting transfers between devices  93.7 us (27%)
  waiting for transfers between devices  75.1 us (22%)
  Pallas kernels  34.6 us (10%)
  between operations  14.4 us (4%)
  local copies, waits for them, and re-layouts  9.08 us (3%)
    all_to_all x1, blocking collectives, local(): tiles = lax.all_to_all(tiles, ('zh', 'heads'), 0, 0, tiled=True)  49 us
    ppermute x6, starting transfers between devices, halo(): return (lax.ppermute(last, NODES, up), lax.ppermute(first, NODES, down))  42 us
    all_to_all x4, blocking collectives, exchange(): return lax.all_to_all(x, 'heads', 0, 0, tiled=True)  39.7 us
    ppermute x6, waiting for transfers between devices, halo(): return (lax.ppermute(last, NODES, up), lax.ppermute(first, NODES, down))  37.5 us
    all_to_all x1, blocking collectives, over_plane(): return lax.all_to_all(x, ('y', 'x'), 0, 0, tiled=True)  26.4 us
    ppermute x6, starting transfers between devices, trade(): out.append(lax.ppermute(parts[k], 'heads', [(i, i ^ k) for i in range(4)]))  22.3 us
    ppermute x6, waiting for transfers between devices, trade(): out.append(lax.ppermute(parts[k], 'heads', [(i, i ^ k) for i in range(4)]))  15.5 us
    ppermute x3, starting transfers between devices, over_cores(): return lax.ppermute(x, 'core', [(0, 1), (1, 0)])  15.2 us
  transfers between devices with their start and end apart: 18, of which 8 were waited for; matrix products, arithmetic and copies ran while one was open for 1% of the time, Pallas kernels for 7%

profile of v2, /device:TPU:31, one launch (start us, length us, event | category | flops | bytes accessed | tf_op | source)
XLA Modules:
  0.0 344.0 jit_solution(9262962554236997349)
XLA Ops:
  7.2 1.8 shard_map.213
  9.0 49.0 %all_to_all.40.src = bf16[16,20,8,128]{3,2,1,0:T(8,128)(2,1)S(1)} all-to-all(bf16[16,20,8,128]{3,2,1,0:T(8,128)(2,1)} %shard_map.213), channel_id=1, replica_groups=mesh['zh'=4,'y'=4,'x'=4,'core'=2,'heads'=4] {'zh','heads'}, dimensions={0} | all-to-all | bytes 1310720 | tf_op jit(solution)/shard_map/all_to_all | solution.py:406
  58.0 1.2 shard_map.214
  59.2 26.4 %all_to_all.41.mine = bf16[16,4,8,1536]{3,2,1,0:T(8,128)(2,1)S(1)} all-to-all(bf16[16,4,8,1536]{3,2,1,0:T(8,128)(2,1)S(1)} %get-tuple-element.20), channel_id=1, replica_groups=mesh['zh'=4,'y'=4,'x'=4,'core'=2,'heads'=4] {'y','x'}, dimensions={0} | all-to-all | bytes 3145728 | tf_op jit(solution)/shard_map/all_to_all | solution.py:365
  85.6 10.9 %collective-permute-start.3 = (bf16[16,4,8,1536]{3,2,1,0:T(8,128)(2,1)S(1)}, bf16[16,4,8,1536]{3,2,1,0:T(8,128)(2,1)S(1)}, u32[]{:S(2)}, u32[]{:S(2)}) collective-permute-start(bf16[16,4,8,1536]{3,2,1,0:T(8,128)(2,1)S(1)} %all_to_all.41.mine), channel_id=1, source_target_pairs={{0,4},{4,0},{1,5},{5,1},{2,6},{6,2},{3,7},{7,3},{8,12},{12,8},{9,1... | collective-permute-start | bytes 4718600 | tf_op jit(solution)/shard_map/ppermute | solution.py:347
  96.6 1.1 dynamic-slice_bitcast_fusion
  97.6 0.7 pad_maximum_fusion
  98.3 4.9 %collective-permute-start = (bf16[320,256]{1,0:T(8,128)(2,1)}, bf16[320,256]{1,0:T(8,128)(2,1)S(1)}, u32[]{:S(2)}, u32[]{:S(2)}) collective-permute-start(bf16[320,256]{1,0:T(8,128)(2,1)} %pad_maximum_fusion), channel_id=1, source_target_pairs={{0,1},{1,0},{2,3},{3,2},{4,5},{5,4},{6,7},{7,6},{8,9},{9,8},{10,11... | collective-permute-start | bytes 491528 | tf_op jit(solution)/shard_map/ppermute | solution.py:353
  103.9 3.6 %collective-permute-start.1 = (bf16[320,256]{1,0:T(8,128)(2,1)}, bf16[320,256]{1,0:T(8,128)(2,1)S(1)}, u32[]{:S(2)}, u32[]{:S(2)}) collective-permute-start(bf16[320,256]{1,0:T(8,128)(2,1)} %pad_maximum_fusion.1), channel_id=1, source_target_pairs={{0,2},{1,3},{2,0},{3,1},{4,6},{5,7},{6,4},{7,5},{8,10},{9,11},{10,... | collective-permute-start | bytes 491528 | tf_op jit(solution)/shard_map/ppermute | solution.py:353
  108.1 2.3 collective-permute-start.2
  110.5 1.0 copy-done.3
  111.6 0.9 copy-done.5
  113.0 6.8 %collective-permute-done.1.x2 = bf16[320,256]{1,0:T(8,128)(2,1)S(1)} collective-permute-done((bf16[320,256]{1,0:T(8,128)(2,1)}, bf16[320,256]{1,0:T(8,128)(2,1)S(1)}, u32[]{:S(2)}, u32[]{:S(2)}) %collective-permute-start.1) | collective-permute-done | bytes 163872 | tf_op jit(solution)/shard_map/ppermute | solution.py:353
  119.9 1.2 copy-done.1
  121.1 1.5 copy-done.2
  122.5 3.3 shard_map.215
  125.8 5.7 %collective-permute-start.4 = (bf16[288,256]{1,0:T(8,128)(2,1)S(1)}, bf16[288,256]{1,0:T(8,128)(2,1)S(1)}, u32[]{:S(2)}, u32[]{:S(2)}) collective-permute-start(bf16[288,256]{1,0:T(8,128)(2,1)S(1)} %get-tuple-element.26), channel_id=1, source_target_pairs={{0,1},{1,0},{2,3},{3,2},{4,5},{5,4},{6,7},{7,6},{8,9},{9,8},{10,11... | collective-permute-start | bytes 442376 | tf_op jit(solution)/shard_map/ppermute | solution.py:353
  131.5 1.9 collective-permute-start.5
  133.5 4.0 %collective-permute-start.6 = (bf16[288,256]{1,0:T(8,128)(2,1)S(1)}, bf16[288,256]{1,0:T(8,128)(2,1)S(1)}, u32[]{:S(2)}, u32[]{:S(2)}) collective-permute-start(bf16[288,256]{1,0:T(8,128)(2,1)S(1)} %get-tuple-element.28), channel_id=1, source_target_pairs={{0,3},{1,2},{2,1},{3,0},{4,7},{5,6},{6,5},{7,4},{8,11},{9,10},{10,... | collective-permute-start | bytes 442376 | tf_op jit(solution)/shard_map/ppermute | solution.py:353
  137.5 8.6 %collective-permute-done.5.x2 = bf16[288,256]{1,0:T(8,128)(2,1)S(1)} collective-permute-done((bf16[288,256]{1,0:T(8,128)(2,1)S(1)}, bf16[288,256]{1,0:T(8,128)(2,1)S(1)}, u32[]{:S(2)}, u32[]{:S(2)}) %collective-permute-start.5) | collective-permute-done | bytes 147488 | tf_op jit(solution)/shard_map/ppermute | solution.py:353
  146.7 7.9 %collective-permute-start.7 = (bf16[2,256,256]{2,1,0:T(8,128)(2,1)S(1)}, bf16[2,256,256]{2,1,0:T(8,128)(2,1)S(1)}, u32[]{:S(2)}, u32[]{:S(2)}) collective-permute-start(bf16[2,256,256]{2,1,0:T(8,128)(2,1)S(1)} %get-tuple-element.30), channel_id=1, source_target_pairs={{0,4},{4,8},{8,12},{12,16},{16,20},{20,24},{24,28},{28,32},{32,36}... | collective-permute-start | bytes 786440 | tf_op jit(solution)/shard_map/ppermute | solution.py:335
  154.6 1.9 collective-permute-start.8
  156.6 1.4 collective-permute-done.7.before
  157.9 16.7 %collective-permute-done.8.after = bf16[2,256,256]{2,1,0:T(8,128)(2,1)S(1)} collective-permute-done((bf16[2,256,256]{2,1,0:T(8,128)(2,1)S(1)}, bf16[2,256,256]{2,1,0:T(8,128)(2,1)S(1)}, u32[]{:S(2)}, u32[]{:S(2)}) %collective-permute-start.8) | collective-permute-done | bytes 262176 | tf_op jit(solution)/shard_map/ppermute | solution.py:335
  174.7 2.6 shard_map.217
  177.3 10.9 %all_to_all.42.encoded = bf16[4,64,128]{2,1,0:T(8,128)(2,1)S(1)} all-to-all(bf16[4,64,128]{2,1,0:T(8,128)(2,1)S(1)} %shard_map.217), channel_id=1, replica_groups=mesh['zh'=4,'y'=4,'x'=4,'core'=2,'heads'=4] {'heads'}, dimensions={0} | all-to-all | bytes 131072 | tf_op jit(solution)/shard_map/all_to_all | solution.py:328
  188.2 1.9 collective-permute-start.9
  190.1 1.7 slice.12
  191.8 2.4 collective-permute-start.10
  194.2 12.9 %collective-permute-done.10.theirs = bf16[16,4,8,2048]{3,2,1,0:T(8,128)(2,1)S(1)} collective-permute-done((bf16[16,4,8,2048]{3,2,1,0:T(8,128)(2,1)S(1)}, bf16[16,4,8,2048]{3,2,1,0:T(8,128)(2,1)S(1)}, u32[]{:S(2)}, u32[]{:S(2)}) %collective-permute-start.10) | collective-permute-done | bytes 2097184 | tf_op jit(solution)/shard_map/ppermute | solution.py:347
  207.2 3.5 %shard_map.219 = (bf16[4,64,384]{2,1,0:T(8,128)(2,1)S(1)}, bf16[64,1024]{1,0:T(8,128)(2,1)S(1)}) custom-call(s32[5]{0:T(128)S(1)} %stack.19.pos, bf16[4,64,128]{2,1,0:T(8,128)(2,1)S(1)} %all_to_all.42.encoded, bf16[4,64,256]{2,1,0:T(8,128)(2,1)S(1)} %get-tuple-element.33.mesh, bf16[16,4,8,8704]{3,2,1,0:T(8,128)(2,1)} %bitcast.33, ...), custom_call_target="tpu_custom_call" | custom-call | flops 268435456 | bytes 1048576 | tf_op jit(solution)/shard_map/pallas_call | solution.py:456
  210.7 8.9 %all_to_all.43.own = bf16[4,64,384]{2,1,0:T(8,128)(2,1)S(1)} all-to-all(bf16[4,64,384]{2,1,0:T(8,128)(2,1)S(1)} %get-tuple-element.34), channel_id=1, replica_groups=mesh['zh'=4,'y'=4,'x'=4,'core'=2,'heads'=4] {'heads'}, dimensions={0} | all-to-all | bytes 393216 | tf_op jit(solution)/shard_map/all_to_all | solution.py:328
  219.6 3.8 %collective-permute-start.12 = (bf16[4,64,256]{2,1,0:T(8,128)(2,1)S(1)}, bf16[4,64,256]{2,1,0:T(8,128)(2,1)S(1)}, u32[]{:S(2)}, u32[]{:S(2)}) collective-permute-start(bf16[4,64,256]{2,1,0:T(8,128)(2,1)S(1)} %slice.16), channel_id=1, source_target_pairs={{4,0},{8,4},{12,8},{16,12},{20,16},{24,20},{28,24},{32,28},{36,32}... | collective-permute-start | bytes 393224 | tf_op jit(solution)/shard_map/ppermute | solution.py:335
  223.4 9.9 %collective-permute-start.11 = (bf16[4,64,256]{2,1,0:T(8,128)(2,1)S(1)}, bf16[4,64,256]{2,1,0:T(8,128)(2,1)S(1)}, u32[]{:S(2)}, u32[]{:S(2)}) collective-permute-start(bf16[4,64,256]{2,1,0:T(8,128)(2,1)S(1)} %slice.16), channel_id=1, source_target_pairs={{0,4},{4,8},{8,12},{12,16},{16,20},{20,24},{24,28},{28,32},{32,36}... | collective-permute-start | bytes 393224 | tf_op jit(solution)/shard_map/ppermute | solution.py:335
  233.3 5.0 %collective-permute-done.12.after = bf16[4,64,256]{2,1,0:T(8,128)(2,1)S(1)} collective-permute-done((bf16[4,64,256]{2,1,0:T(8,128)(2,1)S(1)}, bf16[4,64,256]{2,1,0:T(8,128)(2,1)S(1)}, u32[]{:S(2)}, u32[]{:S(2)}) %collective-permute-start.12) | collective-permute-done | bytes 131104 | tf_op jit(solution)/shard_map/ppermute | solution.py:335
  238.3 2.1 shard_map.220
  240.4 8.4 %all_to_all.44.windowed = bf16[4,64,128]{2,1,0:T(8,128)(2,1)S(1)} all-to-all(bf16[4,64,128]{2,1,0:T(8,128)(2,1)S(1)} %shard_map.220), channel_id=1, replica_groups=mesh['zh'=4,'y'=4,'x'=4,'core'=2,'heads'=4] {'heads'}, dimensions={0} | all-to-all | bytes 131072 | tf_op jit(solution)/shard_map/all_to_all | solution.py:328
  248.9 8.5 %shard_map.221 = (bf16[4,64,256]{2,1,0:T(8,128)(2,1)}, bf16[4,64,1024]{2,1,0:T(8,128)(2,1)S(1)}) custom-call(s32[5]{0:T(128)S(1)} %stack.19.pos, bf16[4,64,128]{2,1,0:T(8,128)(2,1)S(1)} %all_to_all.44.windowed, bf16[64,1024]{1,0:T(8,128)(2,1)S(1)} %get-tuple-element.35.kept, bf16[16,4,8,8704]{3,2,1,0:T(8,128)(2,1)} %bitcast.34, ...), custom_call_target="tpu_custom_call" | custom-call | flops 268435456 | bytes 1048576 | tf_op jit(solution)/shard_map/pallas_call | solution.py:473
  257.4 11.5 %all_to_all.45.own = bf16[4,64,1024]{2,1,0:T(8,128)(2,1)S(1)} all-to-all(bf16[4,64,1024]{2,1,0:T(8,128)(2,1)S(1)} %get-tuple-element.36), channel_id=1, replica_groups=mesh['zh'=4,'y'=4,'x'=4,'core'=2,'heads'=4] {'heads'}, dimensions={0} | all-to-all | bytes 1048576 | tf_op jit(solution)/shard_map/all_to_all | solution.py:328
  269.0 3.3 all-to-all-start.7
  272.3 16.4 %collective-permute-start.13 = (bf16[128,1024]{1,0:T(8,128)(2,1)S(1)}, bf16[128,1024]{1,0:T(8,128)(2,1)S(1)}, u32[]{:S(2)}, u32[]{:S(2)}) collective-permute-start(bf16[128,1024]{1,0:T(8,128)(2,1)S(1)} %bitcast.40), channel_id=1, source_target_pairs={{0,4},{4,8},{8,12},{12,16},{16,20},{20,24},{24,28},{28,32},{32,36}... | collective-permute-start | bytes 786440 | tf_op jit(solution)/shard_map/ppermute | solution.py:335
  288.8 2.1 collective-permute-start.14
  291.0 2.4 shard_map.218.queries
  293.4 14.3 %collective-permute-done.14.after = bf16[128,1024]{1,0:T(8,128)(2,1)S(1)} collective-permute-done((bf16[128,1024]{1,0:T(8,128)(2,1)S(1)}, bf16[128,1024]{1,0:T(8,128)(2,1)S(1)}, u32[]{:S(2)}, u32[]{:S(2)}) %collective-permute-start.14) | collective-permute-done | bytes 262176 | tf_op jit(solution)/shard_map/ppermute | solution.py:335
  307.7 8.0 %shard_map.222 = bf16[4,256,256]{2,1,0:T(8,128)(2,1)} custom-call(s32[5]{0:T(128)S(1)} %stack.19.pos, s32[8,3]{1,0:T(8,128)S(1)} %copy.24.blocks, s32[8]{0:T(128)S(1)} %copy-done.8, bf16[4,256,256]{2,1,0:T(8,128)(2,1)S(1)} %get-tuple-element.23.grid, bf16[256,512]{1,0:T(8,128)(2,1)S(1)} %shard_map.218.queries, bf16[4,64,1024]{2,1,0:T(8,128)(2,1)S(1)} %all_to_all.45.own, ...), custom_call_target="tpu_custom_call" | custom-call | flops 268435456 | bytes 1048576 | tf_op jit(solution)/shard_map/pallas_call | solution.py:491
  315.8 10.8 %all-to-all-start.6 = ((bf16[4,256,256]{2,1,0:T(8,128)(2,1)}), bf16[4,256,256]{2,1,0:T(8,128)(2,1)S(1)}, u32[]{:S(2)}, u32[]{:S(2)}) async-start(bf16[4,256,256]{2,1,0:T(8,128)(2,1)} %shard_map.222), calls=%async_computation.6 | async-start | bytes 1048576 | tf_op jit(solution)/shard_map/all_to_all | solution.py:328
  326.5 9.1 %all-to-all-done.6 = bf16[4,256,256]{2,1,0:T(8,128)(2,1)S(1)} async-done(((bf16[4,256,256]{2,1,0:T(8,128)(2,1)}), bf16[4,256,256]{2,1,0:T(8,128)(2,1)S(1)}, u32[]{:S(2)}, u32[]{:S(2)}) %all-to-all-start.6) | async-done | bytes 524320 | tf_op jit(solution)/shard_map/all_to_all | solution.py:328
  335.7 0.8 copy.27
  (40 shorter events, 3.5 us)
Async XLA Ops:
  7.2 181.0 %all-gather.3.cloned.1.call-start = ((), (), s32[]{:S(2)}) async-start(), calls=%async_computation.8 | async-start | bytes 9469952 | tf_op jit(solution)/shard_map/all_gather | solution.py:412
  59.2 37.3 %copy-start.4 = (bf16[256,256]{1,0:T(8,128)(2,1)S(1)}, bf16[256,256]{1,0:T(8,128)(2,1)}, u32[]{:S(2)}) copy-start(bf16[256,256]{1,0:T(8,128)(2,1)} %param.22) | copy-start | bytes 393220
  85.6 34.3 %collective-permute-start.3 = (bf16[16,4,8,1536]{3,2,1,0:T(8,128)(2,1)S(1)}, bf16[16,4,8,1536]{3,2,1,0:T(8,128)(2,1)S(1)}, u32[]{:S(2)}, u32[]{:S(2)}) collective-permute-start(bf16[16,4,8,1536]{3,2,1,0:T(8,128)(2,1)S(1)} %all_to_all.41.mine), channel_id=1, source_target_pairs={{0,4},{4,0},{1,5},{5,1},{2,6},{6,2},{3,7},{7,3},{8,12},{12,8},{9,1... | collective-permute-start | bytes 4718600 | tf_op jit(solution)/shard_map/ppermute | solution.py:347
  98.3 14.7 %collective-permute-start = (bf16[320,256]{1,0:T(8,128)(2,1)}, bf16[320,256]{1,0:T(8,128)(2,1)S(1)}, u32[]{:S(2)}, u32[]{:S(2)}) collective-permute-start(bf16[320,256]{1,0:T(8,128)(2,1)} %pad_maximum_fusion), channel_id=1, source_target_pairs={{0,1},{1,0},{2,3},{3,2},{4,5},{5,4},{6,7},{7,6},{8,9},{9,8},{10,11... | collective-permute-start | bytes 491528 | tf_op jit(solution)/shard_map/ppermute | solution.py:353
  103.9 16.0 %collective-permute-start.1 = (bf16[320,256]{1,0:T(8,128)(2,1)}, bf16[320,256]{1,0:T(8,128)(2,1)S(1)}, u32[]{:S(2)}, u32[]{:S(2)}) collective-permute-start(bf16[320,256]{1,0:T(8,128)(2,1)} %pad_maximum_fusion.1), channel_id=1, source_target_pairs={{0,2},{1,3},{2,0},{3,1},{4,6},{5,7},{6,4},{7,5},{8,10},{9,11},{10,... | collective-permute-start | bytes 491528 | tf_op jit(solution)/shard_map/ppermute | solution.py:353
  108.1 11.8 %collective-permute-start.2 = (bf16[320,256]{1,0:T(8,128)(2,1)}, bf16[320,256]{1,0:T(8,128)(2,1)}, u32[]{:S(2)}, u32[]{:S(2)}) collective-permute-start(bf16[320,256]{1,0:T(8,128)(2,1)} %pad_maximum_fusion.2), channel_id=1, source_target_pairs={{0,3},{1,2},{2,1},{3,0},{4,7},{5,6},{6,5},{7,4},{8,11},{9,10},{10,... | collective-permute-start | bytes 491528 | tf_op jit(solution)/shard_map/ppermute | solution.py:353
  110.5 1.0 copy-start.3
  111.6 0.9 copy-start.5
  112.5 62.2 %copy-start.6 = (s32[2,8]{1,0:T(2,128)S(1)}, s32[2,8]{1,0:T(2,128)}, u32[]{:S(2)}) copy-start(s32[2,8]{1,0:T(2,128)} %blocks.2) | copy-start | bytes 196
  112.5 62.2 %copy-start.7 = (s32[2]{0:T(128)S(1)}, s32[2]{0:T(128)}, u32[]{:S(2)}) copy-start(s32[2]{0:T(128)} %count.2) | copy-start | bytes 28
  119.9 1.2 copy-start.1
  121.1 1.5 copy-start.2
  125.8 11.6 %collective-permute-start.4 = (bf16[288,256]{1,0:T(8,128)(2,1)S(1)}, bf16[288,256]{1,0:T(8,128)(2,1)S(1)}, u32[]{:S(2)}, u32[]{:S(2)}) collective-permute-start(bf16[288,256]{1,0:T(8,128)(2,1)S(1)} %get-tuple-element.26), channel_id=1, source_target_pairs={{0,1},{1,0},{2,3},{3,2},{4,5},{5,4},{6,7},{7,6},{8,9},{9,8},{10,11... | collective-permute-start | bytes 442376 | tf_op jit(solution)/shard_map/ppermute | solution.py:353
  131.5 14.6 %collective-permute-start.5 = (bf16[288,256]{1,0:T(8,128)(2,1)S(1)}, bf16[288,256]{1,0:T(8,128)(2,1)S(1)}, u32[]{:S(2)}, u32[]{:S(2)}) collective-permute-start(bf16[288,256]{1,0:T(8,128)(2,1)S(1)} %get-tuple-element.27), channel_id=1, source_target_pairs={{0,2},{1,3},{2,0},{3,1},{4,6},{5,7},{6,4},{7,5},{8,10},{9,11},{10,... | collective-permute-start | bytes 442376 | tf_op jit(solution)/shard_map/ppermute | solution.py:353
  133.5 12.6 %collective-permute-start.6 = (bf16[288,256]{1,0:T(8,128)(2,1)S(1)}, bf16[288,256]{1,0:T(8,128)(2,1)S(1)}, u32[]{:S(2)}, u32[]{:S(2)}) collective-permute-start(bf16[288,256]{1,0:T(8,128)(2,1)S(1)} %get-tuple-element.28), channel_id=1, source_target_pairs={{0,3},{1,2},{2,1},{3,0},{4,7},{5,6},{6,5},{7,4},{8,11},{9,10},{10,... | collective-permute-start | bytes 442376 | tf_op jit(solution)/shard_map/ppermute | solution.py:353
  146.7 11.2 %collective-permute-start.7 = (bf16[2,256,256]{2,1,0:T(8,128)(2,1)S(1)}, bf16[2,256,256]{2,1,0:T(8,128)(2,1)S(1)}, u32[]{:S(2)}, u32[]{:S(2)}) collective-permute-start(bf16[2,256,256]{2,1,0:T(8,128)(2,1)S(1)} %get-tuple-element.30), channel_id=1, source_target_pairs={{0,4},{4,8},{8,12},{12,16},{16,20},{20,24},{24,28},{28,32},{32,36}... | collective-permute-start | bytes 786440 | tf_op jit(solution)/shard_map/ppermute | solution.py:335
  154.6 20.0 %collective-permute-start.8 = (bf16[2,256,256]{2,1,0:T(8,128)(2,1)S(1)}, bf16[2,256,256]{2,1,0:T(8,128)(2,1)S(1)}, u32[]{:S(2)}, u32[]{:S(2)}) collective-permute-start(bf16[2,256,256]{2,1,0:T(8,128)(2,1)S(1)} %get-tuple-element.31), channel_id=1, source_target_pairs={{4,0},{8,4},{12,8},{16,12},{20,16},{24,20},{28,24},{32,28},{36,32}... | collective-permute-start | bytes 786440 | tf_op jit(solution)/shard_map/ppermute | solution.py:335
  188.2 60.7 %collective-permute-start.9 = (bf16[16,4,8,8704]{3,2,1,0:T(8,128)(2,1)}, bf16[16,4,8,8704]{3,2,1,0:T(8,128)(2,1)S(1)}, u32[]{:S(2)}, u32[]{:S(2)}) collective-permute-start(bf16[16,4,8,8704]{3,2,1,0:T(8,128)(2,1)} %bitcast.31), channel_id=1, source_target_pairs={{0,4},{4,0},{1,5},{5,1},{2,6},{6,2},{3,7},{7,3},{8,12},{12,8},{9,1... | collective-permute-start | bytes 26738696 | tf_op jit(solution)/shard_map/ppermute | solution.py:347
  191.8 15.3 %collective-permute-start.10 = (bf16[16,4,8,2048]{3,2,1,0:T(8,128)(2,1)S(1)}, bf16[16,4,8,2048]{3,2,1,0:T(8,128)(2,1)S(1)}, u32[]{:S(2)}, u32[]{:S(2)}) collective-permute-start(bf16[16,4,8,2048]{3,2,1,0:T(8,128)(2,1)S(1)} %slice.12), channel_id=1, source_target_pairs={{0,4},{4,0},{1,5},{5,1},{2,6},{6,2},{3,7},{7,3},{8,12},{12,8},{9,1... | collective-permute-start | bytes 6291464 | tf_op jit(solution)/shard_map/ppermute | solution.py:347
  207.2 31.2 %copy-start.9 = (s32[2,4]{1,0:T(2,128)S(1)}, s32[2,4]{1,0:T(2,128)}, u32[]{:S(2)}) copy-start(s32[2,4]{1,0:T(2,128)} %offsets.1) | copy-start | bytes 100
  219.6 18.7 %collective-permute-start.12 = (bf16[4,64,256]{2,1,0:T(8,128)(2,1)S(1)}, bf16[4,64,256]{2,1,0:T(8,128)(2,1)S(1)}, u32[]{:S(2)}, u32[]{:S(2)}) collective-permute-start(bf16[4,64,256]{2,1,0:T(8,128)(2,1)S(1)} %slice.16), channel_id=1, source_target_pairs={{4,0},{8,4},{12,8},{16,12},{20,16},{24,20},{28,24},{32,28},{36,32}... | collective-permute-start | bytes 393224 | tf_op jit(solution)/shard_map/ppermute | solution.py:335
  223.4 14.9 %collective-permute-start.11 = (bf16[4,64,256]{2,1,0:T(8,128)(2,1)S(1)}, bf16[4,64,256]{2,1,0:T(8,128)(2,1)S(1)}, u32[]{:S(2)}, u32[]{:S(2)}) collective-permute-start(bf16[4,64,256]{2,1,0:T(8,128)(2,1)S(1)} %slice.16), channel_id=1, source_target_pairs={{0,4},{4,8},{8,12},{12,16},{16,20},{20,24},{24,28},{28,32},{32,36}... | collective-permute-start | bytes 393224 | tf_op jit(solution)/shard_map/ppermute | solution.py:335
  248.9 8.6 %copy-start = (bf16[16,4,8,8704]{3,2,1,0:T(8,128)(2,1)}, bf16[16,4,8,8704]{3,2,1,0:T(8,128)(2,1)S(1)}, u32[]{:S(2)}) copy-start(bf16[16,4,8,8704]{3,2,1,0:T(8,128)(2,1)S(1)} %collective-permute-done.9.theirs) | copy-start | bytes 26738692
  257.4 33.5 %copy-start.10 = (s32[8,3]{0,1:T(4,128)S(1)}, s32[8,3]{0,1:T(4,128)}, u32[]{:S(2)}) copy-start(s32[8,3]{0,1:T(4,128)} %param.40) | copy-start | bytes 292
  269.0 46.8 %all-to-all-start.7 = ((bf16[4,64,256]{2,1,0:T(8,128)(2,1)}), bf16[4,64,256]{2,1,0:T(8,128)(2,1)S(1)}, u32[]{:S(2)}, u32[]{:S(2)}) async-start(bf16[4,64,256]{2,1,0:T(8,128)(2,1)} %get-tuple-element.37), calls=%async_computation.7 | async-start | bytes 262144 | tf_op jit(solution)/shard_map/all_to_all | solution.py:328
  272.3 21.0 %collective-permute-start.13 = (bf16[128,1024]{1,0:T(8,128)(2,1)S(1)}, bf16[128,1024]{1,0:T(8,128)(2,1)S(1)}, u32[]{:S(2)}, u32[]{:S(2)}) collective-permute-start(bf16[128,1024]{1,0:T(8,128)(2,1)S(1)} %bitcast.40), channel_id=1, source_target_pairs={{0,4},{4,8},{8,12},{12,16},{16,20},{20,24},{24,28},{28,32},{32,36}... | collective-permute-start | bytes 786440 | tf_op jit(solution)/shard_map/ppermute | solution.py:335
  288.8 19.0 %collective-permute-start.14 = (bf16[128,1024]{1,0:T(8,128)(2,1)S(1)}, bf16[128,1024]{1,0:T(8,128)(2,1)S(1)}, u32[]{:S(2)}, u32[]{:S(2)}) collective-permute-start(bf16[128,1024]{1,0:T(8,128)(2,1)S(1)} %bitcast.39), channel_id=1, source_target_pairs={{4,0},{8,4},{12,8},{16,12},{20,16},{24,20},{28,24},{32,28},{36,32}... | collective-permute-start | bytes 786440 | tf_op jit(solution)/shard_map/ppermute | solution.py:335
  291.0 16.8 %copy-start.8 = (s32[8]{0:T(128)S(1)}, s32[8]{0:T(128)}, u32[]{:S(2)}) copy-start(s32[8]{0:T(128)} %count.3) | copy-start | bytes 100
  315.8 19.9 %all-to-all-start.6 = ((bf16[4,256,256]{2,1,0:T(8,128)(2,1)}), bf16[4,256,256]{2,1,0:T(8,128)(2,1)S(1)}, u32[]{:S(2)}, u32[]{:S(2)}) async-start(bf16[4,256,256]{2,1,0:T(8,128)(2,1)} %shard_map.222), calls=%async_computation.6 | async-start | bytes 1048576 | tf_op jit(solution)/shard_map/all_to_all | solution.py:328
Sparse Core Ops, SparseCore 0:
  59.4 85.3 all-gather.2
